TPU v7x, 256 devices: a whole 4x4x8 slice. The times are simulated.
256 devices in a mesh: heads: 4 (over y_hi, core), blk: 64 (over y_lo, z, x).
Axes of the slice: x: 4, y: 4 (y_hi: 2, y_lo: 2; y = y_hi * 2 + y_lo), z: 8, core: 2. Of those that a mesh axis runs over, the one named last changes fastest.
Arguments:
- tokens: bfloat16 [32768, 4096], P(('blk', 'heads')), may hold values from -6 to 6
- w_query: bfloat16 [4096, 2048], P('blk', 'heads'), may hold values from -0.75 to 0.75
- key_value_weight: bfloat16 [4096, 2, 512], P('blk', None, 'heads'), may hold values from -0.75 to 0.75
- w_out: bfloat16 [2048, 4096], P(('heads', 'blk')), may hold values from -0.5 to 0.5
- doc_lengths: int32 [16], replicated, may hold values from 1 to 8192, 32768 in all
Outputs:
- attended: bfloat16 [32768, 4096], P(('blk', 'heads'))
Inputs may be any that keep to these rules, and one draw needn't show every extreme that they name: `doc_lengths`: the 16 lengths sum to 32768; the longest document has exactly 8192 tokens.
All inputs are finite; a program needn't handle non-finite values.
Results may differ from a plain program's by a relative error of at most 0.012.
Values may be sent and summed in bfloat16 or wider, within the bound.
A program may use at most 128 MiB of HBM per device.

v0:
```python
import jax
import jax.numpy as jnp
from jax import lax
from jax.sharding import PartitionSpec as P

HEAD_SIZE = 128


norm_epsilon = 1e-05
rope_base = 500000.0
masked_score = -1e30


def in_one_piece(arrays, axis, dim, along):
    columns = [a.reshape(*a.shape[:along], -1) for a in arrays]
    both = jnp.concatenate(columns, axis=along)
    whole, at, finished = (lax.all_gather(both, axis, axis=dim, tiled=True), 0, [])
    for a, column in zip(arrays, columns):
        piece = whole[..., at : at + column.shape[along]]
        finished.append(piece.reshape(*piece.shape[:along], *a.shape[along:]))
        at += column.shape[along]
    return tuple(finished)


def shifted(value, axis, steps):
    count = lax.axis_size(axis)
    first, last = (max(0, -steps), min(count, count - steps))
    return lax.ppermute(value, axis, [(source, source + steps) for source in range(first, last)])


def locate_documents(positions, doc_lengths):
    ends = jnp.cumsum(doc_lengths)
    after = positions[:, None] >= ends[None, :]
    ident = jnp.sum(after.astype(jnp.int32), axis=1)
    starts = jnp.sum(jnp.where(after, doc_lengths[None, :], 0), axis=1)
    return (ident, starts)


def apply_rotation(values, relative_offset):
    half = values.shape[-1] // 2
    freqs = jnp.power(rope_base, -2.0 * jnp.arange(half, dtype=jnp.float32) / values.shape[-1])
    angle = relative_offset.astype(jnp.float32)[:, None] * freqs[None, :]
    cosine = jnp.cos(angle)[:, None, :]
    sine = jnp.sin(angle)[:, None, :]
    first = values[..., :half]
    second = values[..., half:]
    return jnp.concatenate(
        [first * cosine - second * sine, second * cosine + first * sine], axis=-1
    )


def on_device(tokens, w_query, key_value_weight, w_out, doc_lengths):
    blk_index = lax.axis_index("blk")
    reach = lax.axis_size("blk") // 4
    values = tokens.astype(jnp.float32)
    normalized_input = (
        values * lax.rsqrt(jnp.mean(values * values, axis=1, keepdims=True) + norm_epsilon)
    ).astype(jnp.bfloat16)
    block_input = lax.all_gather(normalized_input, "heads", axis=0, tiled=True)
    block_rows = block_input.shape[0]
    query_cols = w_query.shape[1]
    kv_cols = key_value_weight.shape[2]
    pieces = in_one_piece((w_query, key_value_weight), "blk", 0, 1)
    count = pieces[0].shape[0]
    query_part = jnp.dot(block_input, pieces[0], preferred_element_type=jnp.float32)
    keyval_part = jnp.dot(
        block_input, pieces[1].reshape(count, 2 * kv_cols), preferred_element_type=jnp.float32
    )
    positions = blk_index * block_rows + jnp.arange(block_rows, dtype=jnp.int32)
    ident, starts = locate_documents(positions, doc_lengths)
    relative_offset = positions - starts
    query_heads = query_cols // HEAD_SIZE
    kv_heads = kv_cols // HEAD_SIZE
    head_group = query_heads // kv_heads
    query_rows = apply_rotation(
        query_part.reshape(block_rows, query_heads, HEAD_SIZE), relative_offset
    ).astype(jnp.bfloat16)
    query_rows = query_rows.reshape(block_rows, kv_heads, head_group, HEAD_SIZE)
    rotated_keys = apply_rotation(
        keyval_part[:, :kv_cols].reshape(block_rows, kv_heads, HEAD_SIZE), relative_offset
    ).astype(jnp.bfloat16)
    value_rows = (
        keyval_part[:, kv_cols:].reshape(block_rows, kv_heads, HEAD_SIZE).astype(jnp.bfloat16)
    )
    kv_block = jnp.stack([rotated_keys, value_rows], axis=1)
    scale = HEAD_SIZE ** (-0.5)

    def attend_tile(state, kv_now, distance):
        key_pos = (blk_index - distance) * block_rows + jnp.arange(block_rows, dtype=jnp.int32)
        key_doc, unused_k = locate_documents(key_pos, doc_lengths)
        keep = (
            (key_pos[None, :] >= 0)
            & (key_pos[None, :] <= positions[:, None])
            & (key_doc[None, :] == ident[:, None])
        )
        highest, totals, accum = state
        scores = (
            jnp.einsum(
                "qhgd,khd->hgqk", query_rows, kv_now[:, 0], preferred_element_type=jnp.float32
            )
            * scale
        )
        scores = jnp.where(keep, scores, masked_score)
        new_high = jnp.maximum(highest, jnp.max(scores, axis=-1))
        fading = jnp.exp(highest - new_high)
        probs = jnp.where(keep, jnp.exp(scores - new_high[..., None]), 0.0)
        totals = totals * fading + jnp.sum(probs, axis=-1)
        update = jnp.einsum(
            "hgqk,khd->hgqd",
            probs.astype(jnp.bfloat16),
            kv_now[:, 1],
            preferred_element_type=jnp.float32,
        )
        accum = accum * fading[..., None] + update
        return (new_high, totals, accum)

    initial = (
        jnp.full((kv_heads, head_group, block_rows), masked_score, jnp.float32),
        jnp.zeros((kv_heads, head_group, block_rows), jnp.float32),
        jnp.zeros((kv_heads, head_group, block_rows, HEAD_SIZE), jnp.float32),
    )
    state = attend_tile(initial, kv_block, 0)

    def advance(distance, carry):
        kv_now, inner = carry
        kv_now = shifted(kv_now, "blk", 1)
        return (kv_now, attend_tile(inner, kv_now, distance))

    unused_kv, state = lax.fori_loop(1, reach + 1, advance, (kv_block, state))
    highest, totals, accum = state
    mixed = accum / totals[..., None]
    mixed = mixed.transpose(2, 0, 1, 3).reshape(block_rows, query_cols).astype(jnp.bfloat16)
    head_rows = lax.all_gather(w_out, "blk", axis=0, tiled=True)
    return lax.psum_scatter(
        jnp.dot(mixed, head_rows, preferred_element_type=jnp.float32).astype(jnp.bfloat16),
        "heads",
        scatter_dimension=0,
        tiled=True,
    )


def solution(mesh):
    return jax.shard_map(
        on_device,
        mesh=mesh,
        in_specs=(
            P(("blk", "heads"), None),
            P("blk", "heads"),
            P("blk", None, "heads"),
            P(("heads", "blk"), None),
            P(),
        ),
        out_specs=P(("blk", "heads"), None),
        check_vma=False,
    )
```

profile of v0, /device:TPU:1, one launch (start us, length us, event | category | flops | bytes accessed | tf_op | source)
XLA Modules:
  0.0 733.6 jit_solution(8738411729264827400)
XLA Ops:
  13.8 42.2 %all-gather.4.cloned.1.call-done = bf16[512,4096]{1,0:T(8,128)(2,1)} async-done(((bf16[128,4096]{1,0:T(8,128)(2,1)}), bf16[512,4096]{1,0:T(8,128)(2,1)}) %all-gather.4.cloned.1.call-update) | async-done | bytes 4194320 | tf_op jit(solution)/shard_map/all_gather | solution.py:59
  56.0 262.9 %all-gather.6.cloned.1.call-done = bf16[4096,768]{1,0:T(8,128)(2,1)} async-done(((bf16[64,768]{1,0:T(8,128)(2,1)}), bf16[4096,768]{1,0:T(8,128)(2,1)}) %all-gather.6.cloned.1.call-update) | async-done | bytes 6291472 | tf_op jit(solution)/shard_map/all_gather | solution.py:17
  318.9 4.2 fusion.29
  324.8 5.8 fusion.21
  335.9 211.9 %while.22 = (s32[]{:T(128)}, bf16[512,2,1,128]{3,0,2,1:T(8,128)(2,1)S(1)}, f32[1,4,512]{2,1,0:T(4,128)S(1)}, f32[1,4,512]{2,1,0:T(4,128)S(1)}, f32[1,4,512,128]{...) while((s32[]{:T(128)}, ...), condition=%wide.region_10.11_spmd.clone, body=%wide.region_6.10_spmd.clone.sunk | while | flops 552107520 | bytes 18236672 | solution.py:129
  345.7 4.2 collective-permute-start
  384.4 6.1 collective-permute-done
  398.7 6.4 collective-permute-done
  409.0 4.2 collective-permute-start
  413.7 5.8 collective-permute-done
  423.4 4.2 collective-permute-start
  428.1 4.2 collective-permute-done
  436.3 4.3 collective-permute-start
  441.1 4.3 collective-permute-done
  449.3 5.2 collective-permute-start
  463.0 5.1 collective-permute-start
  475.8 4.7 collective-permute-start
  487.7 11.1 %collective-permute-start = (bf16[512,2,1,128]{3,0,2,1:T(8,128)(2,1)S(1)}, bf16[512,2,1,128]{3,0,2,1:T(8,128)(2,1)S(1)}, u32[]{:S(2)}, u32[]{:S(2)}) collective-permute-start(bf16[512,2,1,128]{3,0,2,1:T(8,128)(2,1)S(1)} %get-tuple-element.421), channel_id=1, source_target_pairs={{0,1},{1,2},{2,3},{3,4},{4,5},{5,6},{6,7},{7,8},{8,9},{9,10},{10,1... | collective-permute-start | bytes 786440 | tf_op jit(solution)/shard_map/while/body/eval_jaxpr/ppermute | solution.py:28
  506.9 5.6 collective-permute-start
  520.2 5.8 collective-permute-start
  534.1 6.3 collective-permute-start
  548.3 70.6 %all-gather.8.cloned.1.call-done = bf16[512,4096]{1,0:T(8,128)(2,1)} async-done(((bf16[8,4096]{1,0:T(8,128)(2,1)}), bf16[512,4096]{1,0:T(8,128)(2,1)}) %all-gather.8.cloned.1.call-update) | async-done | bytes 4194320 | tf_op jit(solution)/shard_map/all_gather | solution.py:133
  618.9 6.5 convolution_convert_fusion
  625.4 101.6 %reduce-scatter.2.cloned.1.call-done = bf16[128,4096]{1,0:T(8,128)(2,1)} async-done(((bf16[512,4096]{1,0:T(8,128)(2,1)}), bf16[128,4096]{1,0:T(8,128)(2,1)}) %reduce-scatter.2.cloned.1.call-update) | async-done | bytes 1048592 | tf_op jit(solution)/shard_map/reduce_scatter | solution.py:134
  (242 shorter events, 137.3 us)
Async XLA Ops:
  6.5 4.1 copy-start.4
  6.5 4.1 copy-start.3
  6.5 5.6 copy-start.5
  6.5 49.5 %all-gather.4.cloned.1.call-start = ((), (), s32[]{:S(2)}) async-start(), calls=%async_computation.1 | async-start | bytes 5242880 | tf_op jit(solution)/shard_map/all_gather | solution.py:59
  10.6 308.3 %all-gather.6.cloned.1.call-start = ((), (), s32[]{:S(2)}) async-start(), calls=%async_computation.2 | async-start | bytes 6389760 | tf_op jit(solution)/shard_map/all_gather | solution.py:17
  11.3 607.6 %all-gather.8.cloned.1.call-start = ((), (), s32[]{:S(2)}) async-start(), calls=%async_computation.3 | async-start | bytes 4259840 | tf_op jit(solution)/shard_map/all_gather | solution.py:133
  12.1 715.0 %reduce-scatter.2.cloned.1.call-start = ((), (), s32[]{:S(2)}) async-start(), calls=%async_computation.4 | async-start | bytes 5242880 | tf_op jit(solution)/shard_map/reduce_scatter | solution.py:134
  331.7 2.3 copy-start.1
  336.1 5.6 collective-permute-start
  345.7 7.6 %collective-permute-start = (bf16[512,2,1,128]{3,0,2,1:T(8,128)(2,1)S(1)}, bf16[512,2,1,128]{3,0,2,1:T(8,128)(2,1)S(1)}, u32[]{:S(2)}, u32[]{:S(2)}) collective-permute-start(bf16[512,2,1,128]{3,0,2,1:T(8,128)(2,1)S(1)} %get-tuple-element.421), channel_id=1, source_target_pairs={{0,1},{1,2},{2,3},{3,4},{4,5},{5,6},{6,7},{7,8},{8,9},{9,10},{10,1... | collective-permute-start | bytes 786440 | tf_op jit(solution)/shard_map/while/body/eval_jaxpr/ppermute | solution.py:28
  357.2 7.1 collective-permute-start
  368.3 7.8 %collective-permute-start = (bf16[512,2,1,128]{3,0,2,1:T(8,128)(2,1)S(1)}, bf16[512,2,1,128]{3,0,2,1:T(8,128)(2,1)S(1)}, u32[]{:S(2)}, u32[]{:S(2)}) collective-permute-start(bf16[512,2,1,128]{3,0,2,1:T(8,128)(2,1)S(1)} %get-tuple-element.421), channel_id=1, source_target_pairs={{0,1},{1,2},{2,3},{3,4},{4,5},{5,6},{6,7},{7,8},{8,9},{9,10},{10,1... | collective-permute-start | bytes 786440 | tf_op jit(solution)/shard_map/while/body/eval_jaxpr/ppermute | solution.py:28
  380.0 10.5 %collective-permute-start = (bf16[512,2,1,128]{3,0,2,1:T(8,128)(2,1)S(1)}, bf16[512,2,1,128]{3,0,2,1:T(8,128)(2,1)S(1)}, u32[]{:S(2)}, u32[]{:S(2)}) collective-permute-start(bf16[512,2,1,128]{3,0,2,1:T(8,128)(2,1)S(1)} %get-tuple-element.421), channel_id=1, source_target_pairs={{0,1},{1,2},{2,3},{3,4},{4,5},{5,6},{6,7},{7,8},{8,9},{9,10},{10,1... | collective-permute-start | bytes 786440 | tf_op jit(solution)/shard_map/while/body/eval_jaxpr/ppermute | solution.py:28
  394.4 10.7 %collective-permute-start = (bf16[512,2,1,128]{3,0,2,1:T(8,128)(2,1)S(1)}, bf16[512,2,1,128]{3,0,2,1:T(8,128)(2,1)S(1)}, u32[]{:S(2)}, u32[]{:S(2)}) collective-permute-start(bf16[512,2,1,128]{3,0,2,1:T(8,128)(2,1)S(1)} %get-tuple-element.421), channel_id=1, source_target_pairs={{0,1},{1,2},{2,3},{3,4},{4,5},{5,6},{6,7},{7,8},{8,9},{9,10},{10,1... | collective-permute-start | bytes 786440 | tf_op jit(solution)/shard_map/while/body/eval_jaxpr/ppermute | solution.py:28
  409.0 10.5 %collective-permute-start = (bf16[512,2,1,128]{3,0,2,1:T(8,128)(2,1)S(1)}, bf16[512,2,1,128]{3,0,2,1:T(8,128)(2,1)S(1)}, u32[]{:S(2)}, u32[]{:S(2)}) collective-permute-start(bf16[512,2,1,128]{3,0,2,1:T(8,128)(2,1)S(1)} %get-tuple-element.421), channel_id=1, source_target_pairs={{0,1},{1,2},{2,3},{3,4},{4,5},{5,6},{6,7},{7,8},{8,9},{9,10},{10,1... | collective-permute-start | bytes 786440 | tf_op jit(solution)/shard_map/while/body/eval_jaxpr/ppermute | solution.py:28
  423.4 8.9 %collective-permute-start = (bf16[512,2,1,128]{3,0,2,1:T(8,128)(2,1)S(1)}, bf16[512,2,1,128]{3,0,2,1:T(8,128)(2,1)S(1)}, u32[]{:S(2)}, u32[]{:S(2)}) collective-permute-start(bf16[512,2,1,128]{3,0,2,1:T(8,128)(2,1)S(1)} %get-tuple-element.421), channel_id=1, source_target_pairs={{0,1},{1,2},{2,3},{3,4},{4,5},{5,6},{6,7},{7,8},{8,9},{9,10},{10,1... | collective-permute-start | bytes 786440 | tf_op jit(solution)/shard_map/while/body/eval_jaxpr/ppermute | solution.py:28
  436.3 9.1 %collective-permute-start = (bf16[512,2,1,128]{3,0,2,1:T(8,128)(2,1)S(1)}, bf16[512,2,1,128]{3,0,2,1:T(8,128)(2,1)S(1)}, u32[]{:S(2)}, u32[]{:S(2)}) collective-permute-start(bf16[512,2,1,128]{3,0,2,1:T(8,128)(2,1)S(1)} %get-tuple-element.421), channel_id=1, source_target_pairs={{0,1},{1,2},{2,3},{3,4},{4,5},{5,6},{6,7},{7,8},{8,9},{9,10},{10,1... | collective-permute-start | bytes 786440 | tf_op jit(solution)/shard_map/while/body/eval_jaxpr/ppermute | solution.py:28
  449.3 9.8 %collective-permute-start = (bf16[512,2,1,128]{3,0,2,1:T(8,128)(2,1)S(1)}, bf16[512,2,1,128]{3,0,2,1:T(8,128)(2,1)S(1)}, u32[]{:S(2)}, u32[]{:S(2)}) collective-permute-start(bf16[512,2,1,128]{3,0,2,1:T(8,128)(2,1)S(1)} %get-tuple-element.421), channel_id=1, source_target_pairs={{0,1},{1,2},{2,3},{3,4},{4,5},{5,6},{6,7},{7,8},{8,9},{9,10},{10,1... | collective-permute-start | bytes 786440 | tf_op jit(solution)/shard_map/while/body/eval_jaxpr/ppermute | solution.py:28
  463.0 8.8 %collective-permute-start = (bf16[512,2,1,128]{3,0,2,1:T(8,128)(2,1)S(1)}, bf16[512,2,1,128]{3,0,2,1:T(8,128)(2,1)S(1)}, u32[]{:S(2)}, u32[]{:S(2)}) collective-permute-start(bf16[512,2,1,128]{3,0,2,1:T(8,128)(2,1)S(1)} %get-tuple-element.421), channel_id=1, source_target_pairs={{0,1},{1,2},{2,3},{3,4},{4,5},{5,6},{6,7},{7,8},{8,9},{9,10},{10,1... | collective-permute-start | bytes 786440 | tf_op jit(solution)/shard_map/while/body/eval_jaxpr/ppermute | solution.py:28
  475.8 8.0 %collective-permute-start = (bf16[512,2,1,128]{3,0,2,1:T(8,128)(2,1)S(1)}, bf16[512,2,1,128]{3,0,2,1:T(8,128)(2,1)S(1)}, u32[]{:S(2)}, u32[]{:S(2)}) collective-permute-start(bf16[512,2,1,128]{3,0,2,1:T(8,128)(2,1)S(1)} %get-tuple-element.421), channel_id=1, source_target_pairs={{0,1},{1,2},{2,3},{3,4},{4,5},{5,6},{6,7},{7,8},{8,9},{9,10},{10,1... | collective-permute-start | bytes 786440 | tf_op jit(solution)/shard_map/while/body/eval_jaxpr/ppermute | solution.py:28
  487.7 15.3 %collective-permute-start = (bf16[512,2,1,128]{3,0,2,1:T(8,128)(2,1)S(1)}, bf16[512,2,1,128]{3,0,2,1:T(8,128)(2,1)S(1)}, u32[]{:S(2)}, u32[]{:S(2)}) collective-permute-start(bf16[512,2,1,128]{3,0,2,1:T(8,128)(2,1)S(1)} %get-tuple-element.421), channel_id=1, source_target_pairs={{0,1},{1,2},{2,3},{3,4},{4,5},{5,6},{6,7},{7,8},{8,9},{9,10},{10,1... | collective-permute-start | bytes 786440 | tf_op jit(solution)/shard_map/while/body/eval_jaxpr/ppermute | solution.py:28
  506.9 9.4 %collective-permute-start = (bf16[512,2,1,128]{3,0,2,1:T(8,128)(2,1)S(1)}, bf16[512,2,1,128]{3,0,2,1:T(8,128)(2,1)S(1)}, u32[]{:S(2)}, u32[]{:S(2)}) collective-permute-start(bf16[512,2,1,128]{3,0,2,1:T(8,128)(2,1)S(1)} %get-tuple-element.421), channel_id=1, source_target_pairs={{0,1},{1,2},{2,3},{3,4},{4,5},{5,6},{6,7},{7,8},{8,9},{9,10},{10,1... | collective-permute-start | bytes 786440 | tf_op jit(solution)/shard_map/while/body/eval_jaxpr/ppermute | solution.py:28
  520.2 9.9 %collective-permute-start = (bf16[512,2,1,128]{3,0,2,1:T(8,128)(2,1)S(1)}, bf16[512,2,1,128]{3,0,2,1:T(8,128)(2,1)S(1)}, u32[]{:S(2)}, u32[]{:S(2)}) collective-permute-start(bf16[512,2,1,128]{3,0,2,1:T(8,128)(2,1)S(1)} %get-tuple-element.421), channel_id=1, source_target_pairs={{0,1},{1,2},{2,3},{3,4},{4,5},{5,6},{6,7},{7,8},{8,9},{9,10},{10,1... | collective-permute-start | bytes 786440 | tf_op jit(solution)/shard_map/while/body/eval_jaxpr/ppermute | solution.py:28
  534.1 9.8 %collective-permute-start = (bf16[512,2,1,128]{3,0,2,1:T(8,128)(2,1)S(1)}, bf16[512,2,1,128]{3,0,2,1:T(8,128)(2,1)S(1)}, u32[]{:S(2)}, u32[]{:S(2)}) collective-permute-start(bf16[512,2,1,128]{3,0,2,1:T(8,128)(2,1)S(1)} %get-tuple-element.421), channel_id=1, source_target_pairs={{0,1},{1,2},{2,3},{3,4},{4,5},{5,6},{6,7},{7,8},{8,9},{9,10},{10,1... | collective-permute-start | bytes 786440 | tf_op jit(solution)/shard_map/while/body/eval_jaxpr/ppermute | solution.py:28
  (2 other events, 2.7 us)
Sparse Core Ops, SparseCore 0:
  10.7 45.2 all-gather.3
  57.8 261.0 all-gather.5
  320.7 298.1 all-gather.7
  625.5 101.4 reduce-scatter.1
where the time goes:
time: 734 us
  waiting for transfers between devices  541 us (74%)
  starting transfers between devices  78.5 us (11%)
  matrix products  63.8 us (9%)
  other arithmetic  32.9 us (4%)
  between operations  13.4 us (2%)
    all_gather x1, waiting for transfers between devices, in_one_piece(): lax.all_gather(both, axis, axis=dim, tiled=True)  263 us
    reduce_scatter x1, waiting for transfers between devices, on_device(): lax.psum_scatter(jnp.dot(mixed, head_rows, preferred_element_type=jnp.flo...  102 us
    ppermute x16, starting transfers between devices, shifted(): lax.ppermute(value, axis, [(source, source + steps) for source in range(f...  78.4 us
    all_gather x1, waiting for transfers between devices, on_device(): head_rows = lax.all_gather(w_out, 'blk', axis=0, tiled=True)  70.6 us
    ppermute x16, waiting for transfers between devices, shifted(): lax.ppermute(value, axis, [(source, source + steps) for source in range(f...  62.8 us
    all_gather x1, waiting for transfers between devices, on_device(): block_input = lax.all_gather(normalized_input, 'heads', axis=0, tiled=True)  42.2 us
    dot_general x17, matrix products, attend_tile(): jnp.einsum('hgqk,khd->hgqd', probs.astype(jnp.bfloat16), kv_now[:, 1], pr...  32.2 us
    reduce_sum x17, other arithmetic, attend_tile(): totals = totals * fading + jnp.sum(probs, axis=-1)  17.7 us
  transfers between devices with their start and end apart: 20, of which 20 were waited for; matrix products, arithmetic and copies ran while one was open for 12% of the time, Pallas kernels for 0%

commit v1 on v0

v1 whole, which is shorter than its diff:
```python
import functools

import jax
import jax.numpy as jnp
from jax import lax
from jax.experimental import pallas as pl
from jax.experimental.pallas import tpu as pltpu
from jax.sharding import PartitionSpec as P

MESH = pl.DeviceIdType.MESH
BF16 = jnp.bfloat16
F32 = jnp.float32

HEAD = 128
QH = 4
BLK = 512
PIECE = 128
WIDTH = 4096
NX, NZ, NYL = 4, 8, 2
norm_epsilon = 1e-05
rope_base = 500000.0
masked_score = -1e30
LOG2E = 1.4426950408889634


class Place:
    def __init__(self):
        h = lax.axis_index("heads")
        b = lax.axis_index("blk")
        self.h, self.b = h, b
        self.yh, self.c = lax.div(h, 2), lax.rem(h, 2)
        self.yl = lax.div(b, NX * NZ)
        self.z = lax.rem(lax.div(b, NX), NZ)
        self.x = lax.rem(b, NX)
        self.row = b - self.x
        self.xs = [lax.rem(self.x + k, NX) for k in range(NX)]
        self.zs = [lax.rem(self.z + k, NZ) for k in range(NZ)]
        self.xp = (h, self.row + self.xs[1])
        self.xm = (h, self.row + self.xs[3])
        base = b - self.z * NX
        self.zp = (h, base + self.zs[1] * NX)
        self.zm = (h, base + self.zs[7] * NX)
        self.yf = (h, lax.rem(b + NX * NZ, 2 * NX * NZ))
        self.core = (h + 1 - 2 * self.c, b)
        y = 2 * self.yh + self.yl
        inner = lax.rem(b, NX * NZ)
        self.yp = self.at_y(lax.rem(y + 1, 4), inner)
        self.ym = self.at_y(lax.rem(y + 3, 4), inner)
        self.far = lax.rem(h + 2, 4)
        self.nextrow = (h, lax.rem(b + NX, 64))
        self.prevrow = (h, lax.rem(b + 60, 64))

    def at_y(self, y, inner):
        return (2 * lax.div(y, 2) + self.c, NX * NZ * lax.rem(y, 2) + inner)


def meet(devices):
    barrier = pltpu.get_barrier_semaphore()
    for device in devices:
        pl.semaphore_signal(barrier, inc=1, device_id=device, device_id_type=MESH)
    pl.semaphore_wait(barrier, len(devices))


class Sends:
    def __init__(self, send_sem, recv_sem):
        self.send_sem, self.recv_sem, self.made = send_sem, recv_sem, []

    def start(self, src, dst, device):
        i = len(self.made)
        copy = pltpu.make_async_remote_copy(
            src_ref=src,
            dst_ref=dst,
            send_sem=self.send_sem.at[i],
            recv_sem=self.recv_sem.at[i],
            device_id=device,
            device_id_type=MESH,
        )
        copy.start()
        self.made.append(copy)
        return copy

    def same(self, ref, device):
        return self.start(ref, ref, device)

    def drain(self):
        for copy in self.made:
            copy.wait_send()


def project_kernel(
    tokens, wq_in, wkv_in, cos, sin, q_out, kv_out,
    xbuf, ra, rb, wq, wkv, acc, copy_sem, send_sem, recv_sem,
):
    p = Place()
    x, z, yl, h = p.x, p.z, p.yl, p.h
    own_q = pltpu.make_async_copy(wq_in, wq.at[yl, z, x], copy_sem.at[0])
    own_kv = pltpu.make_async_copy(wkv_in, wkv.at[yl, z, x], copy_sem.at[1])
    own_q.start()
    own_kv.start()
    meet([p.xp, p.xm, p.zp, p.zm, p.yp, p.ym, p.core])
    s = Sends(send_sem, recv_sem)
    own_kv.wait()
    y_kv = s.same(wkv.at[yl, z, x], p.yf)
    own_q.wait()
    y_q = s.same(wq.at[yl, z, x], p.yf)

    def normalize(i, carry):
        rows = pl.ds(pl.multiple_of(i * 16, 16), 16)
        v = tokens[rows, :].astype(F32)
        mean = jnp.mean(v * v, axis=1, keepdims=True)
        xbuf[h, rows, :] = (v * lax.rsqrt(mean + norm_epsilon)).astype(BF16)
        return carry

    lax.fori_loop(0, PIECE // 16, normalize, 0)

    y_kv.wait_recv()
    ax = (s.same(wkv.at[:, z, x], p.xp), s.same(wkv.at[:, z, x], p.xm))
    y_q.wait_recv()
    bz = (s.same(wq.at[:, z, x], p.zp), s.same(wq.at[:, z, x], p.zm))

    def bx_send(zz):
        return (s.same(wq.at[:, zz, x], p.xp), s.same(wq.at[:, zz, x], p.xm))

    def bx_forward(zz, pair):
        pair[0].wait_recv()
        one = s.same(wq.at[0, zz, p.xs[3]], p.xp)
        pair[1].wait_recv()
        return (one, s.same(wq.at[1, zz, p.xs[1]], p.xm))

    rows0 = bx_send(z)
    act_core = s.same(xbuf.at[h], p.core)
    act = (
        s.start(xbuf.at[h, pl.ds(0, 64)], ra, p.yp),
        s.start(xbuf.at[h, pl.ds(64, 64)], rb, p.ym),
    )

    def z_forward(buf, pair, step, pick):
        pair[0].wait_recv()
        pair[1].wait_recv()
        low, high = p.zs[NZ - step], p.zs[step]
        if step < NZ // 2 - 1:
            return (s.same(pick(buf, None, low), p.zp), s.same(pick(buf, None, high), p.zm))
        return (s.same(pick(buf, 0, low), p.zp), s.same(pick(buf, 1, high), p.zm))

    def pick_b(buf, part, zz):
        return buf.at[:, zz, x] if part is None else buf.at[part, zz, x]

    def pick_a(buf, part, zz):
        return buf.at[:, zz] if part is None else buf.at[part, zz]

    ax[0].wait_recv()
    ax_far0 = s.same(wkv.at[0, z, p.xs[3]], p.xp)
    ax[1].wait_recv()
    ax_far1 = s.same(wkv.at[1, z, p.xs[1]], p.xm)
    bz = z_forward(wq, bz, 1, pick_b)
    rows1 = (bx_send(p.zs[7]), bx_send(p.zs[1]))
    ax_far0.wait_recv()
    ax_far1.wait_recv()
    bz = z_forward(wq, bz, 2, pick_b)
    az = (s.same(pick_a(wkv, None, z), p.zp), s.same(pick_a(wkv, None, z), p.zm))
    rows2 = (bx_send(p.zs[6]), bx_send(p.zs[2]))
    far0 = bx_forward(z, rows0)
    act[0].wait_recv()
    hm = p.ym[0]
    hp = p.yp[0]
    relay0 = s.start(ra, xbuf.at[hm, pl.ds(0, 64)], p.yp)
    act[1].wait_recv()
    relay1 = s.start(rb, xbuf.at[hp, pl.ds(64, 64)], p.ym)
    bz = z_forward(wq, bz, 3, pick_b)
    rows3 = (bx_send(p.zs[5]), bx_send(p.zs[3]))
    far1 = (bx_forward(p.zs[7], rows1[0]), bx_forward(p.zs[1], rows1[1]))
    az = z_forward(wkv, az, 1, pick_a)
    bz[0].wait_recv()
    bz[1].wait_recv()
    rows4 = bx_send(p.zs[4])
    az = z_forward(wkv, az, 2, pick_a)
    far2 = (bx_forward(p.zs[6], rows2[0]), bx_forward(p.zs[2], rows2[1]))
    relay0.wait_recv()
    relay1.wait_recv()
    act_far = s.same(xbuf.at[p.far], p.core)
    az = z_forward(wkv, az, 3, pick_a)
    far3 = (bx_forward(p.zs[5], rows3[0]), bx_forward(p.zs[3], rows3[1]))
    far4 = bx_forward(p.zs[4], rows4)
    for pair in (az, far0, far1[0], far1[1], far2[0], far2[1], far3[0], far3[1], far4):
        pair[0].wait_recv()
        pair[1].wait_recv()
    act_core.wait_recv()
    act_far.wait_recv()

    def multiply(k, carry):
        left = xbuf[:, :, pl.ds(pl.multiple_of(k * 512, 512), 512)].reshape(BLK, 512)
        ky = lax.div(k, 4)
        kz = 2 * lax.rem(k, 4)
        right = wq[ky, pl.ds(kz, 2)].reshape(512, 512)
        acc[:, :512] += jnp.dot(left, right, preferred_element_type=F32)
        right = wkv[ky, pl.ds(kz, 2)].reshape(512, 256)
        acc[:, 512:] += jnp.dot(left, right, preferred_element_type=F32)
        return carry

    acc[...] = jnp.zeros_like(acc)
    lax.fori_loop(0, 8, multiply, 0)

    for t in range(4):
        rows = slice(t * PIECE, (t + 1) * PIECE)
        co, si = cos[rows, :], sin[rows, :]

        def rotated(at):
            v = acc[rows, at : at + HEAD]
            return v * co + pltpu.roll(v, HEAD // 2, 1) * si

        for j in range(QH):
            q_out[j, rows, :] = rotated(j * HEAD).astype(BF16)
        kv_out[:, rows] = rotated(QH * HEAD).T.astype(BF16)
        kv_out[:, BLK + t * PIECE : BLK + (t + 1) * PIECE] = acc[rows, 640:768].astype(BF16)
    s.drain()


def project(tokens, wq, wkv, cos, sin):
    vmem = pl.BlockSpec(memory_space=pltpu.VMEM)
    hbm = pl.BlockSpec(memory_space=pl.ANY)
    return pl.pallas_call(
        project_kernel,
        out_shape=(
            jax.ShapeDtypeStruct((QH, BLK, HEAD), BF16),
            jax.ShapeDtypeStruct((HEAD, 2 * BLK), BF16),
        ),
        in_specs=[vmem, hbm, hbm, vmem, vmem],
        out_specs=(vmem, vmem),
        scratch_shapes=[
            pltpu.VMEM((4, PIECE, WIDTH), BF16),
            pltpu.VMEM((64, WIDTH), BF16),
            pltpu.VMEM((64, WIDTH), BF16),
            pltpu.VMEM((NYL, NZ, NX, 64, 512), BF16),
            pltpu.VMEM((NYL, NZ, NX, 64, 256), BF16),
            pltpu.VMEM((BLK, 768), F32),
            pltpu.SemaphoreType.DMA((2,)),
            pltpu.SemaphoreType.DMA((64,)),
            pltpu.SemaphoreType.DMA((64,)),
        ],
        compiler_params=pltpu.CompilerParams(
            collective_id=1, has_side_effects=True, vmem_limit_bytes=48 << 20
        ),
        name="project",
    )(tokens, wq, wkv, cos, sin)


def attend_kernel(
    q, kv_in, start, wout_in, mixed, wout_out,
    kv, wout, acc, high, copy_sem, send_sem, recv_sem,
):
    p = Place()
    x, z, yl = p.x, p.z, p.yl
    own_kv = pltpu.make_async_copy(kv_in, kv.at[0, x], copy_sem.at[0])
    own_w = pltpu.make_async_copy(wout_in, wout.at[yl, z, x], copy_sem.at[1])
    own_kv.start()
    own_w.start()
    meet([p.xp, p.xm, p.zp, p.zm, p.yf, p.nextrow, p.prevrow])
    s = Sends(send_sem, recv_sem)
    factor = HEAD ** (-0.5) * LOG2E
    lane = lax.broadcasted_iota(jnp.int32, (256, BLK), 1)

    def attend(d, xx, diagonal=False):
        base = p.row * BLK + (xx - NX * d) * BLK
        keys = kv[d, xx, :, 0:BLK]
        vals = jnp.concatenate(
            [kv[d, xx, :, BLK + i * HEAD : BLK + (i + 1) * HEAD] for i in range(4)], axis=0
        )
        vals = jnp.concatenate([vals, jnp.ones((BLK, HEAD), BF16)], axis=1)

        def head(j, carry):
            for half in range(2):
                rows = slice(half * 256, half * 256 + 256)
                score = jnp.dot(q[j, rows, :], keys, preferred_element_type=F32) * factor
                first = start[rows, :] - base
                keep = lane >= jnp.concatenate([first] * 4, axis=1)
                if diagonal:
                    keep &= lane <= lax.broadcasted_iota(jnp.int32, (256, BLK), 0) + half * 256
                score = jnp.where(keep, score, masked_score)
                top = jnp.max(score, axis=1, keepdims=True)
                if diagonal:
                    new = jnp.broadcast_to(top, (256, HEAD))
                else:
                    old = high[j, rows, :]
                    new = jnp.maximum(old, top)
                probs = jnp.exp2(score - jnp.concatenate([new] * 4, axis=1)).astype(BF16)
                update = jnp.dot(probs, vals, preferred_element_type=F32)
                if not diagonal:
                    fade = jnp.exp2(old - new)
                    update += acc[j, rows, :] * jnp.concatenate([fade, fade], axis=1)
                acc[j, rows, :] = update
                high[j, rows, :] = new
            return carry

        lax.fori_loop(0, QH, head, 0)

    def both(ref):
        return (s.same(ref, p.xp), s.same(ref, p.xm))

    own_kv.wait()
    down = s.start(kv.at[0, x], kv.at[1, x], p.nextrow)
    side = {0: both(kv.at[0, x])}
    own_w.wait()
    w_side = both(wout.at[yl, z, x])
    attend(0, x, diagonal=True)

    w_y = []
    far = {}

    def w_up(zz):
        w_y.append(s.same(wout.at[yl, zz], p.yf))

    def take_down(d):
        nonlocal down
        down.wait_recv()
        if d < 4:
            down = s.start(kv.at[d, x], kv.at[d + 1, x], p.nextrow)
        side[d] = both(kv.at[d, x])

    def take_side(d):
        side[d][0].wait_recv()
        one = s.same(kv.at[d, p.xs[3], pl.ds(0, 64)], p.xp)
        side[d][1].wait_recv()
        far[d] = (one, s.same(kv.at[d, p.xs[1], pl.ds(64, 64)], p.xm))

    def take_far(d):
        far[d][0].wait_recv()
        far[d][1].wait_recv()

    def w_forward(step):
        nonlocal w_z
        w_z[0].wait_recv()
        w_z[1].wait_recv()
        low, high_ = p.zs[NZ - step], p.zs[step]
        if step < 3:
            w_z = (s.same(wout.at[yl, low], p.zp), s.same(wout.at[yl, high_], p.zm))
        else:
            w_z = (
                s.same(wout.at[yl, low, pl.ds(0, 2)], p.zp),
                s.same(wout.at[yl, high_, pl.ds(2, 2)], p.zm),
            )
        w_up(low)
        w_up(high_)

    take_down(1)
    attend(1, x)
    take_side(0)
    w_side[0].wait_recv()
    w_far0 = s.same(wout.at[yl, z, p.xs[3], :, pl.ds(0, 2048)], p.xp)
    w_side[1].wait_recv()
    w_far1 = s.same(wout.at[yl, z, p.xs[1], :, pl.ds(2048, 2048)], p.xm)
    take_down(2)
    attend(2, x)
    w_far0.wait_recv()
    w_far1.wait_recv()
    w_z = (s.same(wout.at[yl, z], p.zp), s.same(wout.at[yl, z], p.zm))
    w_up(z)
    take_side(1)
    attend(1, p.xs[3])
    take_down(3)
    attend(1, p.xs[1])
    attend(3, x)
    take_side(2)
    w_forward(1)
    attend(2, p.xs[3])
    take_far(1)
    attend(1, p.xs[2])
    take_down(4)
    attend(2, p.xs[1])
    take_far(2)
    attend(2, p.xs[2])
    w_forward(2)
    take_side(3)
    attend(4, x)
    attend(3, p.xs[3])
    attend(3, p.xs[1])
    w_forward(3)
    take_side(4)
    take_far(3)
    attend(3, p.xs[2])
    take_far(0)

    def edge(k):
        xx = p.xs[k]
        attend(4 * lax.div(xx - x + 3, 4), xx)

    edge(3)
    edge(1)
    w_z[0].wait_recv()
    w_z[1].wait_recv()
    w_up(p.zs[4])
    take_far(4)
    edge(2)

    for j in range(QH):
        for t in range(4):
            rows = slice(t * PIECE, (t + 1) * PIECE)
            mixed[rows, j * HEAD : (j + 1) * HEAD] = (
                acc[j, rows, :HEAD] / acc[j, rows, HEAD:]
            ).astype(BF16)
    for copy in w_y:
        copy.wait_recv()
    out = pltpu.make_async_copy(wout, wout_out, copy_sem.at[2])
    out.start()
    s.drain()
    out.wait()


def attend_all(q, kv, start, wout):
    vmem = pl.BlockSpec(memory_space=pltpu.VMEM)
    hbm = pl.BlockSpec(memory_space=pl.ANY)
    return pl.pallas_call(
        attend_kernel,
        out_shape=(
            jax.ShapeDtypeStruct((BLK, QH * HEAD), BF16),
            jax.ShapeDtypeStruct((NYL, NZ, NX, 8, WIDTH), BF16),
        ),
        in_specs=[vmem, hbm, vmem, hbm],
        out_specs=(vmem, hbm),
        scratch_shapes=[
            pltpu.VMEM((5, NX, HEAD, 2 * BLK), BF16),
            pltpu.VMEM((NYL, NZ, NX, 8, WIDTH), BF16),
            pltpu.VMEM((QH, BLK, 2 * HEAD), F32),
            pltpu.VMEM((QH, BLK, HEAD), F32),
            pltpu.SemaphoreType.DMA((3,)),
            pltpu.SemaphoreType.DMA((64,)),
            pltpu.SemaphoreType.DMA((64,)),
        ],
        compiler_params=pltpu.CompilerParams(
            collective_id=2, has_side_effects=True, vmem_limit_bytes=48 << 20
        ),
        name="attend",
    )(q, kv, start, wout)


def on_device(tokens, w_query, key_value_weight, w_out, doc_lengths):
    blk_index = lax.axis_index("blk")
    positions = blk_index * BLK + jnp.arange(BLK, dtype=jnp.int32)
    ends = jnp.cumsum(doc_lengths)
    after = positions[:, None] >= ends[None, :]
    starts = jnp.sum(jnp.where(after, doc_lengths[None, :], 0), axis=1).astype(jnp.int32)
    half = HEAD // 2
    freqs = jnp.power(rope_base, -2.0 * jnp.arange(half, dtype=F32) / HEAD)
    angle = (positions - starts).astype(F32)[:, None] * freqs[None, :]
    cosine, sine = jnp.cos(angle), jnp.sin(angle)
    cos2 = jnp.concatenate([cosine, cosine], axis=1)
    sin2 = jnp.concatenate([-sine, sine], axis=1)
    start_rows = jnp.broadcast_to(starts[:, None], (BLK, HEAD))
    q, kv = project(tokens, w_query, key_value_weight.reshape(64, 256), cos2, sin2)
    mixed, head_rows = attend_all(q, kv, start_rows, w_out)
    return lax.psum_scatter(
        jnp.dot(
            mixed, head_rows.reshape(512, WIDTH), preferred_element_type=F32
        ).astype(BF16),
        "heads",
        scatter_dimension=0,
        tiled=True,
    )


def solution(mesh):
    return jax.shard_map(
        on_device,
        mesh=mesh,
        in_specs=(
            P(("blk", "heads"), None),
            P("blk", "heads"),
            P("blk", None, "heads"),
            P(("heads", "blk"), None),
            P(),
        ),
        out_specs=P(("blk", "heads"), None),
        check_vma=False,
    )
```

time: 734 us -> 212 us (0.29)
  waiting for transfers between devices: 541 us -> 60 us
  Pallas kernels: 0 us -> 128 us
  starting transfers between devices: 78.5 us -> 0.01 us
  matrix products: 63.8 us -> 4.28 us
  other arithmetic: 32.9 us -> 2.11 us
    all_gather x3 -> x0, waiting for transfers between devices: 376 us -> none  [the longest x1 263 us: in_one_piece(): lax.all_gather(both, axis, axis=dim, tiled=True)]
    pallas_call x0 -> x2, Pallas kernels: none -> 128 us  [the longest x1 75.5 us: attend_all(): pl.pallas_call(attend_kernel, out_shape=(jax.ShapeDtypeStruct((BLK, QH *...]
    ppermute x16 -> x0, starting transfers between devices: 78.4 us -> none  [shifted(): lax.ppermute(value, axis, [(source, source + steps) for source in range(f...]
    ppermute x16 -> x0, waiting for transfers between devices: 62.8 us -> none  [shifted(): lax.ppermute(value, axis, [(source, source + steps) for source in range(f...]
    dot_general x37 -> x1, matrix products: 63.8 us -> 4.28 us  [on_device(): jnp.dot(mixed, head_rows.reshape(512, WIDTH), preferred_element_type=F32)]
    reduce_scatter x1, waiting for transfers between devices: 102 us -> 60 us  [on_device(): lax.psum_scatter(jnp.dot(mixed, head_rows.reshape(512, WIDTH), preferred_...]
    reduce_sum x35 -> x1, other arithmetic: 20.8 us -> 0.74 us  [on_device(): jnp.sum(jnp.where(after, doc_lengths[None, :], 0), axis=1).astype(jnp.int32)]
  transfers between devices with their start and end apart: 20 -> 1, of which waited for: 20 -> 1; matrix products, arithmetic and copies ran while one was open for 12% -> 0% of each run, Pallas kernels for 0% -> 0%
where the time goes in v1:
time: 212 us
  Pallas kernels  128 us (60%)
  waiting for transfers between devices  60 us (28%)
  between operations  13.5 us (6%)
  matrix products  4.28 us (2%)
  local copies, waits for them, and re-layouts  3.68 us (2%)
    pallas_call x1, Pallas kernels, attend_all(): pl.pallas_call(attend_kernel, out_shape=(jax.ShapeDtypeStruct((BLK, QH *...  75.5 us
    reduce_scatter x1, waiting for transfers between devices, on_device(): lax.psum_scatter(jnp.dot(mixed, head_rows.reshape(512, WIDTH), preferred_...  60 us
    pallas_call x1, Pallas kernels, project(): pl.pallas_call(project_kernel, out_shape=(jax.ShapeDtypeStruct((QH, BLK,...  52.8 us
    dot_general x1, matrix products, on_device(): jnp.dot(mixed, head_rows.reshape(512, WIDTH), preferred_element_type=F32)  4.28 us
  transfers between devices with their start and end apart: 1, of which 1 were waited for; matrix products, arithmetic and copies ran while one was open for 0% of the time, Pallas kernels for 0%

profile of v1, /device:TPU:1, one launch (start us, length us, event | category | flops | bytes accessed | tf_op | source)
XLA Modules:
  0.0 211.9 jit_solution(774991883134519544)
XLA Ops:
  6.5 0.0 copy-start.2
  6.5 0.0 reduce-scatter.2.cloned.1.call-start
  6.6 0.7 copy.8
  7.3 0.1 reduce
  7.5 0.7 select_reduce_fusion
  8.2 0.8 copy.11
  9.0 1.0 fusion
  10.0 0.2 pad_maximum_fusion
  10.2 0.0 copy-start
  10.2 1.2 copy-done
  11.4 0.0 copy-start.1
  11.4 0.8 copy-done.1
  12.2 52.8 %project.1 = (bf16[4,512,128]{2,1,0:T(8,128)(2,1)S(1)}, bf16[128,1024]{1,0:T(8,128)(2,1)S(1)}) custom-call(bf16[128,4096]{1,0:T(8,128)(2,1)S(1)} %copy-done, bf16[64,512]{1,0:T(8,128)(2,1)S(1)} %copy-done.1, bf16[64,256]{1,0:T(8,128)(2,1)S(1)} %bitcast.8, f32[512,128]{1,0:T(8,128)S(1)} %get-tuple-element.16.cos, f32[512,128]{1,0:T(8,128)S(1)} %get-tuple-element.17.sin), custom_call_target="tpu_custom_call" | custom-call | tf_op jit(solution)/shard_map/project/pallas_call | solution.py:221
  65.1 0.1 broadcast_in_dim.16.start
  65.2 0.0 copy-done.2
  65.2 75.5 %attend.1 = (bf16[512,512]{1,0:T(8,128)(2,1)S(1)}, bf16[2,8,4,8,4096]{4,3,2,1,0:T(8,128)(2,1)S(1)}) custom-call(bf16[4,512,128]{2,1,0:T(8,128)(2,1)S(1)} %get-tuple-element.9.q, bf16[128,1024]{1,0:T(8,128)(2,1)S(1)} %get-tuple-element.10.kv_in, s32[512,128]{1,0:T(8,128)S(1)} %broadcast_in_dim.16.start, bf16[8,4096]{1,0:T(8,128)(2,1)S(1)} %copy-done.2), custom_call_target="tpu_custom_call" | custom-call | tf_op jit(solution)/shard_map/attend/pallas_call | solution.py:411
  140.7 4.3 %convolution_convert_fusion = bf16[512,4096]{1,0:T(8,128)(2,1)} fusion(bf16[512,512]{1,0:T(8,128)(2,1)S(1)} %get-tuple-element.11, bf16[512,4096]{1,0:T(8,128)(2,1)S(1)} %bitcast.9), kind=kOutput, calls=%fused_computation | convolution fusion | flops 2149580800 | bytes 8912896 | tf_op jit(solution)/shard_map/dot_general | solution.py:451
  145.0 0.0 reduce-scatter.2.cloned.1.call-update
  145.0 60.0 %reduce-scatter.2.cloned.1.call-done = bf16[128,4096]{1,0:T(8,128)(2,1)} async-done(((bf16[512,4096]{1,0:T(8,128)(2,1)}), bf16[128,4096]{1,0:T(8,128)(2,1)}) %reduce-scatter.2.cloned.1.call-update) | async-done | bytes 1048592 | tf_op jit(solution)/shard_map/reduce_scatter | solution.py:450
  (4 shorter events, 0.1 us)
Async XLA Ops:
  6.5 58.7 %copy-start.2 = (bf16[8,4096]{1,0:T(8,128)(2,1)S(1)}, bf16[8,4096]{1,0:T(8,128)(2,1)}, u32[]{:S(2)}) copy-start(bf16[8,4096]{1,0:T(8,128)(2,1)} %wout_in.1) | copy-start | bytes 196612
  6.5 198.5 %reduce-scatter.2.cloned.1.call-start = ((), (), s32[]{:S(2)}) async-start(), calls=%async_computation.1 | async-start | bytes 5242880 | tf_op jit(solution)/shard_map/reduce_scatter | solution.py:450
  10.2 1.2 copy-start
  11.4 0.8 copy-start.1
Sparse Core Ops, SparseCore 0:
  145.2 59.8 reduce-scatter.1

commit v2 on v1

--- a/solution.py
+++ b/solution.py
@@ -245,8 +245,8 @@
 
 
 def attend_kernel(
-    q, kv_in, start, wout_in, mixed, wout_out,
-    kv, wout, acc, high, copy_sem, send_sem, recv_sem,
+    q, kv_in, start, wout_in, mixed, wout,
+    kv, acc, high, copy_sem, send_sem, recv_sem,
 ):
     p = Place()
     x, z, yl = p.x, p.z, p.yl
@@ -399,10 +399,7 @@
             ).astype(BF16)
     for copy in w_y:
         copy.wait_recv()
-    out = pltpu.make_async_copy(wout, wout_out, copy_sem.at[2])
-    out.start()
     s.drain()
-    out.wait()
 
 
 def attend_all(q, kv, start, wout):
@@ -415,13 +412,12 @@
             jax.ShapeDtypeStruct((NYL, NZ, NX, 8, WIDTH), BF16),
         ),
         in_specs=[vmem, hbm, vmem, hbm],
-        out_specs=(vmem, hbm),
+        out_specs=(vmem, vmem),
         scratch_shapes=[
             pltpu.VMEM((5, NX, HEAD, 2 * BLK), BF16),
-            pltpu.VMEM((NYL, NZ, NX, 8, WIDTH), BF16),
             pltpu.VMEM((QH, BLK, 2 * HEAD), F32),
             pltpu.VMEM((QH, BLK, HEAD), F32),
-            pltpu.SemaphoreType.DMA((3,)),
+            pltpu.SemaphoreType.DMA((2,)),
             pltpu.SemaphoreType.DMA((64,)),
             pltpu.SemaphoreType.DMA((64,)),
         ],
@@ -430,6 +426,81 @@
         ),
         name="attend",
     )(q, kv, start, wout)
+
+
+NCHUNK, CHUNK = 8, 512
+
+
+def output_kernel(
+    mixed, w, out, give_far, take_far, own_far, sum_far, via, got, give_near, take_near, own,
+    send_sem, recv_sem,
+):
+    p = Place()
+    other = p.h + 1 - 2 * p.c
+    far_other = lax.rem(other + 2, 4)
+    meet([p.yp, p.ym, p.core])
+    s = Sends(send_sem, recv_sem)
+
+    def times(owner, n):
+        rows = pl.ds(pl.multiple_of(owner * PIECE, PIECE), PIECE)
+        return jnp.dot(
+            mixed[rows, :], w[:, n * CHUNK : (n + 1) * CHUNK], preferred_element_type=F32
+        )
+
+    def toward(n):
+        return p.yp if n % 2 == 0 else p.ym
+
+    to_core, hops, near = [], [], []
+
+    def combine(n):
+        to_core[n].wait_recv()
+        sum_far[n] = (own_far[n] + take_far[n].astype(F32)).astype(BF16)
+        hops.append(s.start(sum_far.at[n], via.at[n], toward(n)))
+
+    for n in range(NCHUNK):
+        give_far[n] = times(far_other, n).astype(BF16)
+        to_core.append(s.start(give_far.at[n], take_far.at[n], p.core))
+        own_far[n] = times(p.far, n)
+        if n >= 2:
+            combine(n - 2)
+    combine(NCHUNK - 2)
+    combine(NCHUNK - 1)
+    for n in range(NCHUNK):
+        give_near[n] = times(other, n).astype(BF16)
+        near.append(s.start(give_near.at[n], take_near.at[n], p.core))
+        own[n] = times(p.h, n)
+    last = []
+    for n in range(NCHUNK):
+        hops[n].wait_recv()
+        last.append(s.start(via.at[n], got.at[n], toward(n)))
+    for n in range(NCHUNK):
+        near[n].wait_recv()
+        own[n] += take_near[n].astype(F32)
+    for n in range(NCHUNK):
+        last[n].wait_recv()
+        out[:, n * CHUNK : (n + 1) * CHUNK] = (own[n] + got[n].astype(F32)).astype(BF16)
+    s.drain()
+
+
+def project_out(mixed, w):
+    vmem = pl.BlockSpec(memory_space=pltpu.VMEM)
+    piece = pltpu.VMEM((NCHUNK, PIECE, CHUNK), BF16)
+    wide = pltpu.VMEM((NCHUNK, PIECE, CHUNK), F32)
+    return pl.pallas_call(
+        output_kernel,
+        out_shape=jax.ShapeDtypeStruct((PIECE, WIDTH), BF16),
+        in_specs=[vmem, vmem],
+        out_specs=vmem,
+        scratch_shapes=[
+            piece, piece, wide, piece, piece, piece, piece, piece, wide,
+            pltpu.SemaphoreType.DMA((32,)),
+            pltpu.SemaphoreType.DMA((32,)),
+        ],
+        compiler_params=pltpu.CompilerParams(
+            collective_id=3, has_side_effects=True, vmem_limit_bytes=48 << 20
+        ),
+        name="output",
+    )(mixed, w)
 
 
 def on_device(tokens, w_query, key_value_weight, w_out, doc_lengths):
@@ -447,14 +518,7 @@
     start_rows = jnp.broadcast_to(starts[:, None], (BLK, HEAD))
     q, kv = project(tokens, w_query, key_value_weight.reshape(64, 256), cos2, sin2)
     mixed, head_rows = attend_all(q, kv, start_rows, w_out)
-    return lax.psum_scatter(
-        jnp.dot(
-            mixed, head_rows.reshape(512, WIDTH), preferred_element_type=F32
-        ).astype(BF16),
-        "heads",
-        scatter_dimension=0,
-        tiled=True,
-    )
+    return project_out(mixed, head_rows.reshape(512, WIDTH))
 
 
 def solution(mesh):

time: 212 us -> 172 us (0.81)
  waiting for transfers between devices: 60 us -> 0 us
  Pallas kernels: 128 us -> 165 us
  between operations: 13.5 us -> 0.07 us
  matrix products: 4.28 us -> 0 us
    reduce_scatter x1 -> x0, waiting for transfers between devices: 60 us -> none  [on_device(): lax.psum_scatter(jnp.dot(mixed, head_rows.reshape(512, WIDTH), preferred_...]
    pallas_call x0 -> x1, Pallas kernels: none -> 37.3 us  [project_out(): pl.pallas_call(output_kernel, out_shape=jax.ShapeDtypeStruct((PIECE, WIDT...]
    dot_general x1 -> x0, matrix products: 4.28 us -> none  [on_device(): jnp.dot(mixed, head_rows.reshape(512, WIDTH), preferred_element_type=F32)]
  transfers between devices with their start and end apart: 1 -> 0, of which waited for: 1 -> 0; matrix products, arithmetic and copies ran while one was open for 0% -> 0% of each run, Pallas kernels for 0% -> 0%
where the time goes in v2:
time: 172 us
  Pallas kernels  165 us (96%)
  local copies, waits for them, and re-layouts  4.68 us (3%)
  other arithmetic  2.12 us (1%)
    pallas_call x1, Pallas kernels, attend_all(): pl.pallas_call(attend_kernel, out_shape=(jax.ShapeDtypeStruct((BLK, QH *...  75.2 us
    pallas_call x1, Pallas kernels, project(): pl.pallas_call(project_kernel, out_shape=(jax.ShapeDtypeStruct((QH, BLK,...  52.8 us
    pallas_call x1, Pallas kernels, project_out(): pl.pallas_call(output_kernel, out_shape=jax.ShapeDtypeStruct((PIECE, WIDT...  37.3 us
    unnamed x8, local copies, waits for them, and re-layouts  3.8 us

profile of v2, /device:TPU:1, one launch (start us, length us, event | category | flops | bytes accessed | tf_op | source)
XLA Modules:
  0.0 172.2 jit_solution(16431374384505878099)
XLA Ops:
  0.0 0.0 copy-start.2
  0.0 0.8 copy.8
  0.8 0.1 reduce
  0.9 0.7 select_reduce_fusion
  1.7 0.8 copy.11
  2.5 0.1 broadcast_in_dim.16.start
  2.6 1.0 fusion
  3.6 0.2 pad_maximum_fusion
  3.8 0.0 copy-start
  3.8 1.2 copy-done
  5.0 0.0 copy-start.1
  5.0 0.8 copy-done.1
  5.9 52.8 %project.1 = (bf16[4,512,128]{2,1,0:T(8,128)(2,1)S(1)}, bf16[128,1024]{1,0:T(8,128)(2,1)S(1)}) custom-call(bf16[128,4096]{1,0:T(8,128)(2,1)S(1)} %copy-done, bf16[64,512]{1,0:T(8,128)(2,1)S(1)} %copy-done.1, bf16[64,256]{1,0:T(8,128)(2,1)S(1)} %bitcast.7, f32[512,128]{1,0:T(8,128)S(1)} %get-tuple-element.16.cos, f32[512,128]{1,0:T(8,128)S(1)} %get-tuple-element.17.sin), custom_call_target="tpu_custom_call" | custom-call | tf_op jit(solution)/shard_map/project/pallas_call | solution.py:221
  58.7 0.0 copy-done.2
  58.7 75.2 %attend.1 = (bf16[512,512]{1,0:T(8,128)(2,1)S(1)}, bf16[2,8,4,8,4096]{4,3,2,1,0:T(8,128)(2,1)S(1)}) custom-call(bf16[4,512,128]{2,1,0:T(8,128)(2,1)S(1)} %get-tuple-element.9.q, bf16[128,1024]{1,0:T(8,128)(2,1)S(1)} %get-tuple-element.10.kv_in, s32[512,128]{1,0:T(8,128)S(1)} %broadcast_in_dim.16.start, bf16[8,4096]{1,0:T(8,128)(2,1)S(1)} %copy-done.2), custom_call_target="tpu_custom_call" | custom-call | tf_op jit(solution)/shard_map/attend/pallas_call | solution.py:408
  133.9 37.3 %output.1 = bf16[128,4096]{1,0:T(8,128)(2,1)S(1)} custom-call(bf16[512,512]{1,0:T(8,128)(2,1)S(1)} %get-tuple-element.11.mixed, bf16[512,4096]{1,0:T(8,128)(2,1)S(1)} %bitcast.6), custom_call_target="tpu_custom_call" | custom-call | tf_op jit(solution)/shard_map/output/pallas_call | solution.py:489
  171.2 1.0 copy.13
  (4 shorter events, 0.1 us)
Async XLA Ops:
  0.0 58.7 %copy-start.2 = (bf16[8,4096]{1,0:T(8,128)(2,1)S(1)}, bf16[8,4096]{1,0:T(8,128)(2,1)}, u32[]{:S(2)}) copy-start(bf16[8,4096]{1,0:T(8,128)(2,1)} %wout_in.1) | copy-start | bytes 196612
  3.8 1.2 copy-start
  5.0 0.8 copy-start.1

commit v3 on v2

v3 whole, which is shorter than its diff:
```python
import functools

import jax
import jax.numpy as jnp
from jax import lax
from jax.experimental import pallas as pl
from jax.experimental.pallas import tpu as pltpu
from jax.sharding import PartitionSpec as P

MESH = pl.DeviceIdType.MESH
BF16 = jnp.bfloat16
F32 = jnp.float32

HEAD = 128
QH = 4
BLK = 512
PIECE = 128
WIDTH = 4096
NX, NZ, NYL = 4, 8, 2
norm_epsilon = 1e-05
rope_base = 500000.0
masked_score = -1e30
LOG2E = 1.4426950408889634


class Place:
    def __init__(self):
        h = lax.axis_index("heads")
        b = lax.axis_index("blk")
        self.h, self.b = h, b
        self.yh, self.c = lax.div(h, 2), lax.rem(h, 2)
        self.yl = lax.div(b, NX * NZ)
        self.z = lax.rem(lax.div(b, NX), NZ)
        self.x = lax.rem(b, NX)
        self.row = b - self.x
        self.xs = [lax.rem(self.x + k, NX) for k in range(NX)]
        self.zs = [lax.rem(self.z + k, NZ) for k in range(NZ)]
        self.xp = (h, self.row + self.xs[1])
        self.xm = (h, self.row + self.xs[3])
        base = b - self.z * NX
        self.zp = (h, base + self.zs[1] * NX)
        self.zm = (h, base + self.zs[7] * NX)
        self.yf = (h, lax.rem(b + NX * NZ, 2 * NX * NZ))
        self.core = (h + 1 - 2 * self.c, b)
        y = 2 * self.yh + self.yl
        inner = lax.rem(b, NX * NZ)
        self.yp = self.at_y(lax.rem(y + 1, 4), inner)
        self.ym = self.at_y(lax.rem(y + 3, 4), inner)
        self.far = lax.rem(h + 2, 4)
        self.nextrow = (h, lax.rem(b + NX, 64))
        self.prevrow = (h, lax.rem(b + 60, 64))

    def at_y(self, y, inner):
        return (2 * lax.div(y, 2) + self.c, NX * NZ * lax.rem(y, 2) + inner)


def meet(devices):
    barrier = pltpu.get_barrier_semaphore()
    for device in devices:
        pl.semaphore_signal(barrier, inc=1, device_id=device, device_id_type=MESH)
    pl.semaphore_wait(barrier, len(devices))


class Sends:
    def __init__(self, send_sem, recv_sem):
        self.send_sem, self.recv_sem, self.made = send_sem, recv_sem, []

    def start(self, src, dst, device):
        i = len(self.made)
        copy = pltpu.make_async_remote_copy(
            src_ref=src,
            dst_ref=dst,
            send_sem=self.send_sem.at[i],
            recv_sem=self.recv_sem.at[i],
            device_id=device,
            device_id_type=MESH,
        )
        copy.start()
        self.made.append(copy)
        return copy

    def same(self, ref, device):
        return self.start(ref, ref, device)

    def drain(self):
        for copy in self.made:
            copy.wait_send()


FACTOR = HEAD ** (-0.5) * LOG2E


def attention_kernel(
    tokens_in, wq_in, wkv_in, wout_in, cos, sin, start, mixed, wout,
    tokens, xbuf, ra, rb, wq, wkv, raw, qt, kv, acc, high, copy_sem, send_sem, recv_sem,
):
    p = Place()
    x, z, yl, h = p.x, p.z, p.yl, p.h
    own = [
        pltpu.make_async_copy(wkv_in, wkv.at[yl, z, x], copy_sem.at[0]),
        pltpu.make_async_copy(wq_in, wq.at[yl, z, x], copy_sem.at[1]),
        pltpu.make_async_copy(tokens_in, tokens, copy_sem.at[2]),
        pltpu.make_async_copy(wout_in, wout.at[yl, z, x], copy_sem.at[3]),
    ]
    for copy in own:
        copy.start()
    meet([p.xp, p.xm, p.zp, p.zm, p.yp, p.ym, p.core, p.nextrow, p.prevrow])
    s = Sends(send_sem, recv_sem)

    def both(ref):
        return (s.same(ref, p.xp), s.same(ref, p.xm))

    def settle(pair):
        pair[0].wait_recv()
        pair[1].wait_recv()

    own[0].wait()
    y_kv = s.same(wkv.at[yl, z, x], p.yf)
    own[1].wait()
    y_q = s.same(wq.at[yl, z, x], p.yf)
    own[2].wait()

    def normalize(i, carry):
        rows = pl.ds(pl.multiple_of(i * 16, 16), 16)
        v = tokens[rows, :].astype(F32)
        mean = jnp.mean(v * v, axis=1, keepdims=True)
        xbuf[h, rows, :] = (v * lax.rsqrt(mean + norm_epsilon)).astype(BF16)
        return carry

    lax.fori_loop(0, PIECE // 16, normalize, 0)

    def bx_send(zz):
        return both(wq.at[:, zz, x])

    def bx_forward(zz, pair):
        pair[0].wait_recv()
        one = s.same(wq.at[0, zz, p.xs[3]], p.xp)
        pair[1].wait_recv()
        return (one, s.same(wq.at[1, zz, p.xs[1]], p.xm))

    def z_forward(pair, step, pick):
        settle(pair)
        low, high_ = p.zs[NZ - step], p.zs[step]
        if step < NZ // 2 - 1:
            return (s.same(pick(None, low), p.zp), s.same(pick(None, high_), p.zm))
        return (s.same(pick(0, low), p.zp), s.same(pick(1, high_), p.zm))

    def pick_b(part, zz):
        return wq.at[:, zz, x] if part is None else wq.at[part, zz, x]

    def pick_a(part, zz):
        return wkv.at[:, zz] if part is None else wkv.at[part, zz]

    def pick_w(part, zz):
        return wout.at[yl, zz] if part is None else wout.at[yl, zz, pl.ds(2 * part, 2)]

    y_kv.wait_recv()
    ax = both(wkv.at[:, z, x])
    y_q.wait_recv()
    bz = (s.same(wq.at[:, z, x], p.zp), s.same(wq.at[:, z, x], p.zm))
    rows0 = bx_send(z)
    act_core = s.same(xbuf.at[h], p.core)
    act = (
        s.start(xbuf.at[h, pl.ds(0, 64)], ra, p.yp),
        s.start(xbuf.at[h, pl.ds(64, 64)], rb, p.ym),
    )
    ax[0].wait_recv()
    ax_far0 = s.same(wkv.at[0, z, p.xs[3]], p.xp)
    ax[1].wait_recv()
    ax_far = (ax_far0, s.same(wkv.at[1, z, p.xs[1]], p.xm))
    bz = z_forward(bz, 1, pick_b)
    rows1 = (bx_send(p.zs[7]), bx_send(p.zs[1]))
    settle(ax_far)
    az = (s.same(pick_a(None, z), p.zp), s.same(pick_a(None, z), p.zm))
    bz = z_forward(bz, 2, pick_b)
    rows2 = (bx_send(p.zs[6]), bx_send(p.zs[2]))
    far0 = bx_forward(z, rows0)
    own[3].wait()
    w_side = both(wout.at[yl, z, x])
    act[0].wait_recv()
    relay0 = s.start(ra, xbuf.at[p.ym[0], pl.ds(0, 64)], p.yp)
    act[1].wait_recv()
    relay1 = s.start(rb, xbuf.at[p.yp[0], pl.ds(64, 64)], p.ym)
    az = z_forward(az, 1, pick_a)
    bz = z_forward(bz, 3, pick_b)
    rows3 = (bx_send(p.zs[5]), bx_send(p.zs[3]))
    far1 = (bx_forward(p.zs[7], rows1[0]), bx_forward(p.zs[1], rows1[1]))
    w_side[0].wait_recv()
    w_far0 = s.same(wout.at[yl, z, p.xs[3], :, pl.ds(0, 2048)], p.xp)
    w_side[1].wait_recv()
    w_far = (w_far0, s.same(wout.at[yl, z, p.xs[1], :, pl.ds(2048, 2048)], p.xm))
    az = z_forward(az, 2, pick_a)
    settle(bz)
    rows4 = bx_send(p.zs[4])
    far2 = (bx_forward(p.zs[6], rows2[0]), bx_forward(p.zs[2], rows2[1]))
    settle((relay0, relay1))
    act_far = s.same(xbuf.at[p.far], p.core)
    az = z_forward(az, 3, pick_a)
    settle(w_far)
    w_y = []

    def w_up(zz):
        w_y.append(s.same(wout.at[yl, zz], p.yf))

    w_z = (s.same(pick_w(None, z), p.zp), s.same(pick_w(None, z), p.zm))
    w_up(z)

    def w_forward(step):
        nonlocal w_z
        w_z = z_forward(w_z, step, pick_w)
        w_up(p.zs[NZ - step])
        w_up(p.zs[step])

    far3 = (bx_forward(p.zs[5], rows3[0]), bx_forward(p.zs[3], rows3[1]))
    settle(az)
    settle((act_core, act_far))

    def left_of(k):
        return xbuf[:, :, pl.ds(pl.multiple_of(k * 512, 512), 512)].reshape(BLK, 512)

    def multiply_kv(k, carry):
        right = wkv[lax.div(k, 4), pl.ds(2 * lax.rem(k, 4), 2)].reshape(512, 256)
        raw[:, 512:] += jnp.dot(left_of(k), right, preferred_element_type=F32)
        return carry

    def multiply_q(k, carry):
        right = wq[lax.div(k, 4), pl.ds(2 * lax.rem(k, 4), 2)].reshape(512, 512)
        raw[:, :512] += jnp.dot(left_of(k), right, preferred_element_type=F32)
        return carry

    def rotated(rows, at):
        v = raw[rows, at : at + HEAD]
        return v * cos[rows, :] + pltpu.roll(v, HEAD // 2, 1) * sin[rows, :]

    raw[...] = jnp.zeros_like(raw)
    lax.fori_loop(0, 8, multiply_kv, 0)
    for t in range(4):
        rows = slice(t * PIECE, (t + 1) * PIECE)
        kv[0, x, :, rows] = raw[rows, 640:768].T.astype(BF16)
        kv[0, x, :, BLK + t * PIECE : BLK + (t + 1) * PIECE] = rotated(rows, 512).astype(BF16)
    far4 = bx_forward(p.zs[4], rows4)
    down = s.start(kv.at[0, x], kv.at[1, x], p.nextrow)
    side = {0: both(kv.at[0, x])}
    far = {}

    for pair in (far0, far1[0], far1[1], far2[0], far2[1], far3[0], far3[1], far4):
        settle(pair)
    lax.fori_loop(0, 8, multiply_q, 0)
    for j in range(QH):
        for t in range(4):
            rows = slice(t * PIECE, (t + 1) * PIECE)
            qt[:, j * BLK + t * PIECE : j * BLK + (t + 1) * PIECE] = (
                (rotated(rows, j * HEAD) * FACTOR).T.astype(BF16)
            )

    key_at = lax.broadcasted_iota(jnp.int32, (BLK, BLK), 0)

    def attend(d, xx, diagonal=False):
        first = start[...] - (p.row + xx - NX * d) * BLK
        keys = jnp.concatenate(
            [kv[d, xx, :, BLK + i * HEAD : BLK + (i + 1) * HEAD] for i in range(4)], axis=0
        )
        vals = jnp.concatenate([kv[d, xx, :, :BLK], jnp.ones((16, BLK), BF16)], axis=0)

        def scores(j):
            return jnp.dot(
                keys, qt[:, j * BLK : (j + 1) * BLK], preferred_element_type=F32
            )

        def finish(j, score):
            at = slice(j * BLK, (j + 1) * BLK)
            keep = key_at >= first
            if diagonal:
                keep &= key_at <= lax.broadcasted_iota(jnp.int32, (BLK, BLK), 1)
            score = jnp.where(keep, score, masked_score)
            new = jnp.max(score, axis=0, keepdims=True)
            if not diagonal:
                old = high[:, at]
                new = jnp.maximum(old, new)
            probs = jnp.exp2(score - new).astype(BF16)
            update = jnp.dot(vals, probs, preferred_element_type=F32)
            if not diagonal:
                update += acc[:, at] * jnp.exp2(old - new)
            acc[:, at] = update
            high[:, at] = new

        now = scores(0)
        for j in range(QH):
            later = scores(j + 1) if j + 1 < QH else None
            finish(j, now)
            now = later

    def take_down(d):
        nonlocal down
        down.wait_recv()
        if d < 4:
            down = s.start(kv.at[d, x], kv.at[d + 1, x], p.nextrow)
        side[d] = both(kv.at[d, x])

    def take_side(d):
        side[d][0].wait_recv()
        one = s.same(kv.at[d, p.xs[3], pl.ds(0, 64)], p.xp)
        side[d][1].wait_recv()
        far[d] = (one, s.same(kv.at[d, p.xs[1], pl.ds(64, 64)], p.xm))

    def take_far(d):
        settle(far[d])

    w_forward(1)
    attend(0, x, diagonal=True)
    take_down(1)
    take_side(0)
    attend(1, x)
    w_forward(2)
    take_down(2)
    attend(2, x)
    take_side(1)
    attend(1, p.xs[3])
    attend(1, p.xs[1])
    take_down(3)
    attend(3, x)
    w_forward(3)
    take_side(2)
    take_far(1)
    attend(1, p.xs[2])
    attend(2, p.xs[3])
    attend(2, p.xs[1])
    take_down(4)
    attend(4, x)
    take_side(3)
    take_far(2)
    attend(2, p.xs[2])
    settle(w_z)
    w_up(p.zs[4])
    attend(3, p.xs[3])
    attend(3, p.xs[1])
    take_side(4)
    take_far(3)
    attend(3, p.xs[2])
    take_far(0)

    def edge(k):
        xx = p.xs[k]
        attend(4 * lax.div(xx - x + 3, 4), xx)

    edge(3)
    edge(1)
    take_far(4)
    edge(2)

    for j in range(QH):
        for t in range(4):
            at = slice(j * BLK + t * PIECE, j * BLK + (t + 1) * PIECE)
            part = acc[:HEAD, at] * (1.0 / acc[HEAD : HEAD + 1, at])
            mixed[t * PIECE : (t + 1) * PIECE, j * HEAD : (j + 1) * HEAD] = part.T.astype(BF16)
    for copy in w_y:
        copy.wait_recv()
    s.drain()


def attention(tokens, wq, wkv, wout, cos, sin, start):
    vmem = pl.BlockSpec(memory_space=pltpu.VMEM)
    hbm = pl.BlockSpec(memory_space=pltpu.HBM)
    return pl.pallas_call(
        attention_kernel,
        out_shape=(
            jax.ShapeDtypeStruct((BLK, QH * HEAD), BF16),
            jax.ShapeDtypeStruct((NYL, NZ, NX, 8, WIDTH), BF16),
        ),
        in_specs=[hbm, hbm, hbm, hbm, vmem, vmem, vmem],
        out_specs=(vmem, vmem),
        scratch_shapes=[
            pltpu.VMEM((PIECE, WIDTH), BF16),
            pltpu.VMEM((4, PIECE, WIDTH), BF16),
            pltpu.VMEM((64, WIDTH), BF16),
            pltpu.VMEM((64, WIDTH), BF16),
            pltpu.VMEM((NYL, NZ, NX, 64, 512), BF16),
            pltpu.VMEM((NYL, NZ, NX, 64, 256), BF16),
            pltpu.VMEM((BLK, 768), F32),
            pltpu.VMEM((HEAD, QH * BLK), BF16),
            pltpu.VMEM((5, NX, HEAD, 2 * BLK), BF16),
            pltpu.VMEM((HEAD + 16, QH * BLK), F32),
            pltpu.VMEM((1, QH * BLK), F32),
            pltpu.SemaphoreType.DMA((4,)),
            pltpu.SemaphoreType.DMA((112,)),
            pltpu.SemaphoreType.DMA((112,)),
        ],
        compiler_params=pltpu.CompilerParams(
            collective_id=1, has_side_effects=True, vmem_limit_bytes=36 << 20
        ),
        name="attention",
    )(tokens, wq, wkv, wout, cos, sin, start)


NCHUNK, CHUNK = 8, 512


def output_kernel(
    mixed, w, out, give_far, take_far, own_far, sum_far, via, got, give_near, take_near, own,
    send_sem, recv_sem,
):
    p = Place()
    other = p.h + 1 - 2 * p.c
    far_other = lax.rem(other + 2, 4)
    meet([p.yp, p.ym, p.core])
    s = Sends(send_sem, recv_sem)

    def times(owner, n):
        rows = pl.ds(pl.multiple_of(owner * PIECE, PIECE), PIECE)
        return jnp.dot(
            mixed[rows, :], w[:, n * CHUNK : (n + 1) * CHUNK], preferred_element_type=F32
        )

    def toward(n):
        return p.yp if n % 2 == 0 else p.ym

    to_core, hops, near = [], [], []

    def combine(n):
        to_core[n].wait_recv()
        sum_far[n] = (own_far[n] + take_far[n].astype(F32)).astype(BF16)
        hops.append(s.start(sum_far.at[n], via.at[n], toward(n)))

    for n in range(NCHUNK):
        give_far[n] = times(far_other, n).astype(BF16)
        to_core.append(s.start(give_far.at[n], take_far.at[n], p.core))
        own_far[n] = times(p.far, n)
        if n >= 2:
            combine(n - 2)
    combine(NCHUNK - 2)
    combine(NCHUNK - 1)
    for n in range(NCHUNK):
        give_near[n] = times(other, n).astype(BF16)
        near.append(s.start(give_near.at[n], take_near.at[n], p.core))
        own[n] = times(p.h, n)
    last = []
    for n in range(NCHUNK):
        hops[n].wait_recv()
        last.append(s.start(via.at[n], got.at[n], toward(n)))
    for n in range(NCHUNK):
        near[n].wait_recv()
        own[n] += take_near[n].astype(F32)
    for n in range(NCHUNK):
        last[n].wait_recv()
        out[:, n * CHUNK : (n + 1) * CHUNK] = (own[n] + got[n].astype(F32)).astype(BF16)
    s.drain()


def project_out(mixed, w):
    vmem = pl.BlockSpec(memory_space=pltpu.VMEM)
    piece = pltpu.VMEM((NCHUNK, PIECE, CHUNK), BF16)
    wide = pltpu.VMEM((NCHUNK, PIECE, CHUNK), F32)
    return pl.pallas_call(
        output_kernel,
        out_shape=jax.ShapeDtypeStruct((PIECE, WIDTH), BF16),
        in_specs=[vmem, vmem],
        out_specs=vmem,
        scratch_shapes=[
            piece, piece, wide, piece, piece, piece, piece, piece, wide,
            pltpu.SemaphoreType.DMA((32,)),
            pltpu.SemaphoreType.DMA((32,)),
        ],
        compiler_params=pltpu.CompilerParams(
            collective_id=3, has_side_effects=True, vmem_limit_bytes=48 << 20
        ),
        name="output",
    )(mixed, w)


def on_device(tokens, w_query, key_value_weight, w_out, doc_lengths):
    blk_index = lax.axis_index("blk")
    positions = blk_index * BLK + jnp.arange(BLK, dtype=jnp.int32)
    ends = jnp.cumsum(doc_lengths)
    after = positions[:, None] >= ends[None, :]
    starts = jnp.sum(jnp.where(after, doc_lengths[None, :], 0), axis=1).astype(jnp.int32)
    half = HEAD // 2
    freqs = jnp.power(rope_base, -2.0 * jnp.arange(half, dtype=F32) / HEAD)
    angle = (positions - starts).astype(F32)[:, None] * freqs[None, :]
    cosine, sine = jnp.cos(angle), jnp.sin(angle)
    cos2 = jnp.concatenate([cosine, cosine], axis=1)
    sin2 = jnp.concatenate([-sine, sine], axis=1)
    mixed, head_rows = attention(
        tokens, w_query, key_value_weight.reshape(64, 256), w_out, cos2, sin2, starts[None, :]
    )
    return project_out(mixed, head_rows.reshape(512, WIDTH))


def solution(mesh):
    return jax.shard_map(
        on_device,
        mesh=mesh,
        in_specs=(
            P(("blk", "heads"), None),
            P("blk", "heads"),
            P("blk", None, "heads"),
            P(("heads", "blk"), None),
            P(),
        ),
        out_specs=P(("blk", "heads"), None),
        check_vma=False,
    )
```

time: 172 us -> 154 us (0.90)
  Pallas kernels: 165 us -> 146 us
    pallas_call x2 -> x1, Pallas kernels: 128 us -> 112 us  [attention(): pl.pallas_call(attention_kernel, out_shape=(jax.ShapeDtypeStruct((BLK, QH...]
    pallas_call x1, Pallas kernels: 37.3 us -> 33.8 us  [project_out(): pl.pallas_call(output_kernel, out_shape=jax.ShapeDtypeStruct((PIECE, WIDT...]
where the time goes in v3:
time: 154 us; the launch traced here: 153 us
  Pallas kernels  146 us (95%)
  local copies, waits for them, and re-layouts  5.37 us (3%)
  other arithmetic  2.11 us (1%)
    pallas_call x1, Pallas kernels, attention(): pl.pallas_call(attention_kernel, out_shape=(jax.ShapeDtypeStruct((BLK, QH...  112 us
    pallas_call x1, Pallas kernels, project_out(): pl.pallas_call(output_kernel, out_shape=jax.ShapeDtypeStruct((PIECE, WIDT...  33.8 us
    unnamed x8, local copies, waits for them, and re-layouts  4.64 us

profile of v3, /device:TPU:1, one launch (start us, length us, event | category | flops | bytes accessed | tf_op | source)
XLA Modules:
  0.0 153.4 jit_solution(14084881723870810900)
XLA Ops:
  0.0 0.7 copy.8
  0.8 0.1 reduce
  0.9 0.7 select_reduce_fusion
  1.7 0.8 copy.11
  2.4 1.0 fusion
  3.4 0.2 pad_maximum_fusion
  3.6 0.0 copy-start
  3.7 1.2 copy-done
  4.9 0.0 copy-start.1
  4.9 0.8 copy-done.1
  5.7 0.0 copy-start.2
  5.7 0.8 copy-done.2
  6.5 112.1 %attention.1 = (bf16[512,512]{1,0:T(8,128)(2,1)S(1)}, bf16[2,8,4,8,4096]{4,3,2,1,0:T(8,128)(2,1)S(1)}) custom-call(bf16[128,4096]{1,0:T(8,128)(2,1)S(1)} %copy-done, bf16[64,512]{1,0:T(8,128)(2,1)S(1)} %copy-done.1, bf16[64,256]{1,0:T(8,128)(2,1)S(1)} %bitcast.8, bf16[8,4096]{1,0:T(8,128)(2,1)S(1)} %copy-done.2, f32[512,128]{1,0:T(8,128)S(1)} %get-tuple-element.12.cos, ...), custom_call_target="tpu_custom_call" | custom-call | tf_op jit(solution)/shard_map/attention/pallas_call | solution.py:364
  118.6 33.8 %output.1 = bf16[128,4096]{1,0:T(8,128)(2,1)S(1)} custom-call(bf16[512,512]{1,0:T(8,128)(2,1)S(1)} %get-tuple-element.7.mixed, bf16[512,4096]{1,0:T(8,128)(2,1)S(1)} %bitcast.7), custom_call_target="tpu_custom_call" | custom-call | tf_op jit(solution)/shard_map/output/pallas_call | solution.py:453
  152.4 1.0 copy.13
  (4 shorter events, 0.1 us)
Async XLA Ops:
  3.6 1.2 copy-start
  4.9 0.8 copy-start.1
  5.7 0.8 copy-start.2

commit v4 on v3

--- a/solution.py
+++ b/solution.py
@@ -63,11 +63,12 @@
 
 class Sends:
     def __init__(self, send_sem, recv_sem):
-        self.send_sem, self.recv_sem, self.made = send_sem, recv_sem, []
-
-    def start(self, src, dst, device):
-        i = len(self.made)
-        copy = pltpu.make_async_remote_copy(
+        self.send_sem, self.recv_sem, self.made, self.count = send_sem, recv_sem, [], 0
+
+    def make(self, src, dst, device):
+        i = self.count
+        self.count += 1
+        return pltpu.make_async_remote_copy(
             src_ref=src,
             dst_ref=dst,
             send_sem=self.send_sem.at[i],
@@ -75,6 +76,9 @@
             device_id=device,
             device_id_type=MESH,
         )
+
+    def start(self, src, dst, device):
+        copy = self.make(src, dst, device)
         copy.start()
         self.made.append(copy)
         return copy
@@ -90,9 +94,11 @@
 FACTOR = HEAD ** (-0.5) * LOG2E
 
 
-def attention_kernel(
-    tokens_in, wq_in, wkv_in, wout_in, cos, sin, start, mixed, wout,
-    tokens, xbuf, ra, rb, wq, wkv, raw, qt, kv, acc, high, copy_sem, send_sem, recv_sem,
+def layer_kernel(
+    docs, tokens_in, wq_in, wkv_in, wout_in, freqs, out,
+    tokens, xbuf, ra, rb, wq, wkv, wout, cos, sin, start, raw, qt, kv, acc, high,
+    w, mixed, give_far, take_far, own_far, sum_far, via, got, give_near, take_near, near_sum,
+    copy_sem, send_sem, recv_sem,
 ):
     p = Place()
     x, z, yl, h = p.x, p.z, p.yl, p.h
@@ -138,24 +144,23 @@
         pair[1].wait_recv()
         return (one, s.same(wq.at[1, zz, p.xs[1]], p.xm))
 
-    def z_forward(pair, step, pick):
-        settle(pair)
-        low, high_ = p.zs[NZ - step], p.zs[step]
-        if step < NZ // 2 - 1:
-            return (s.same(pick(None, low), p.zp), s.same(pick(None, high_), p.zm))
-        return (s.same(pick(0, low), p.zp), s.same(pick(1, high_), p.zm))
-
-    def pick_b(part, zz):
-        return wq.at[:, zz, x] if part is None else wq.at[part, zz, x]
-
-    def pick_a(part, zz):
-        return wkv.at[:, zz] if part is None else wkv.at[part, zz]
-
-    def pick_w(part, zz):
-        return wout.at[yl, zz] if part is None else wout.at[yl, zz, pl.ds(2 * part, 2)]
+    def z_forward(pair, step, ref_of):
+        pair[1].wait_recv()
+        above = s.same(ref_of(p.zs[step]), p.zm)
+        pair[0].wait_recv()
+        below = s.same(ref_of(p.zs[NZ - step]), p.zp) if step < 3 else None
+        return (below, above)
+
+    def pick_b(zz):
+        return wq.at[:, zz, x]
+
+    def pick_a(zz):
+        return wkv.at[:, zz]
 
     y_kv.wait_recv()
     ax = both(wkv.at[:, z, x])
+    own[3].wait()
+    w_side = both(wout.at[yl, z, x])
     y_q.wait_recv()
     bz = (s.same(wq.at[:, z, x], p.zp), s.same(wq.at[:, z, x], p.zm))
     rows0 = bx_send(z)
@@ -164,56 +169,88 @@
         s.start(xbuf.at[h, pl.ds(0, 64)], ra, p.yp),
         s.start(xbuf.at[h, pl.ds(64, 64)], rb, p.ym),
     )
+    def first_of(position):
+        first, end = jnp.zeros_like(position), 0
+        for k in range(docs.shape[0]):
+            end = end + docs[k]
+            first = jnp.where(position >= end, end, first)
+        return first
+
+    start[...] = first_of(p.b * BLK + lax.broadcasted_iota(jnp.int32, (1, BLK), 1))
+
+    def turn(t, carry):
+        rows = pl.ds(pl.multiple_of(t * 64, 64), 64)
+        position = p.b * BLK + t * 64 + lax.broadcasted_iota(jnp.int32, (64, HEAD), 0)
+        angle = (position - first_of(position)).astype(F32) * freqs[...]
+        cos[rows, :] = jnp.cos(angle)
+        sine = jnp.sin(angle)
+        left = lax.broadcasted_iota(jnp.int32, (64, HEAD), 1) < HEAD // 2
+        sin[rows, :] = jnp.where(left, -sine, sine)
+        return carry
+
+    lax.fori_loop(0, BLK // 64, turn, 0)
+
     ax[0].wait_recv()
     ax_far0 = s.same(wkv.at[0, z, p.xs[3]], p.xp)
     ax[1].wait_recv()
     ax_far = (ax_far0, s.same(wkv.at[1, z, p.xs[1]], p.xm))
+    w_side[0].wait_recv()
+    w_far0 = s.same(wout.at[yl, z, p.xs[3], :, pl.ds(0, 2048)], p.xp)
+    w_side[1].wait_recv()
+    w_far = (w_far0, s.same(wout.at[yl, z, p.xs[1], :, pl.ds(2048, 2048)], p.xm))
     bz = z_forward(bz, 1, pick_b)
     rows1 = (bx_send(p.zs[7]), bx_send(p.zs[1]))
     settle(ax_far)
-    az = (s.same(pick_a(None, z), p.zp), s.same(pick_a(None, z), p.zm))
+    az = (s.same(pick_a(z), p.zp), s.same(pick_a(z), p.zm))
+    settle(w_far)
+    w_y = []
+
+    def w_up(zz):
+        w_y.append(s.same(wout.at[yl, zz], p.yf))
+
+    def w_from_below(step):
+        nonlocal w_below
+        w_below.wait_recv()
+        zz = p.zs[NZ - step]
+        if step < 3:
+            w_below = s.same(wout.at[yl, zz], p.zp)
+        w_up(zz)
+
     bz = z_forward(bz, 2, pick_b)
     rows2 = (bx_send(p.zs[6]), bx_send(p.zs[2]))
     far0 = bx_forward(z, rows0)
-    own[3].wait()
-    w_side = both(wout.at[yl, z, x])
     act[0].wait_recv()
     relay0 = s.start(ra, xbuf.at[p.ym[0], pl.ds(0, 64)], p.yp)
     act[1].wait_recv()
     relay1 = s.start(rb, xbuf.at[p.yp[0], pl.ds(64, 64)], p.ym)
+    w_up(z)
     az = z_forward(az, 1, pick_a)
+    w_below = s.same(wout.at[yl, z], p.zp)
     bz = z_forward(bz, 3, pick_b)
     rows3 = (bx_send(p.zs[5]), bx_send(p.zs[3]))
     far1 = (bx_forward(p.zs[7], rows1[0]), bx_forward(p.zs[1], rows1[1]))
-    w_side[0].wait_recv()
-    w_far0 = s.same(wout.at[yl, z, p.xs[3], :, pl.ds(0, 2048)], p.xp)
-    w_side[1].wait_recv()
-    w_far = (w_far0, s.same(wout.at[yl, z, p.xs[1], :, pl.ds(2048, 2048)], p.xm))
     az = z_forward(az, 2, pick_a)
-    settle(bz)
+    w_from_below(1)
+    bz[1].wait_recv()
     rows4 = bx_send(p.zs[4])
     far2 = (bx_forward(p.zs[6], rows2[0]), bx_forward(p.zs[2], rows2[1]))
     settle((relay0, relay1))
     act_far = s.same(xbuf.at[p.far], p.core)
     az = z_forward(az, 3, pick_a)
-    settle(w_far)
-    w_y = []
-
-    def w_up(zz):
-        w_y.append(s.same(wout.at[yl, zz], p.yf))
-
-    w_z = (s.same(pick_w(None, z), p.zp), s.same(pick_w(None, z), p.zm))
-    w_up(z)
-
-    def w_forward(step):
-        nonlocal w_z
-        w_z = z_forward(w_z, step, pick_w)
-        w_up(p.zs[NZ - step])
-        w_up(p.zs[step])
+    w_above = s.same(wout.at[yl, z], p.zm)
+
+    def w_from_above(step):
+        nonlocal w_above
+        w_above.wait_recv()
+        zz = p.zs[step]
+        if step < 4:
+            w_above = s.same(wout.at[yl, zz], p.zm)
+        w_up(zz)
 
     far3 = (bx_forward(p.zs[5], rows3[0]), bx_forward(p.zs[3], rows3[1]))
-    settle(az)
+    az[1].wait_recv()
     settle((act_core, act_far))
+    w_from_below(2)
 
     def left_of(k):
         return xbuf[:, :, pl.ds(pl.multiple_of(k * 512, 512), 512)].reshape(BLK, 512)
@@ -240,8 +277,41 @@
         kv[0, x, :, BLK + t * PIECE : BLK + (t + 1) * PIECE] = rotated(rows, 512).astype(BF16)
     far4 = bx_forward(p.zs[4], rows4)
     down = s.start(kv.at[0, x], kv.at[1, x], p.nextrow)
-    side = {0: both(kv.at[0, x])}
-    far = {}
+    side, far = {}, {}
+    inner = (x >= 1) & (x <= 2)
+    first_row = (x <= 2, x >= 1, x == 0, x == 3, x >= 2)
+    last_row = (x >= 1, x <= 2, x == 3, x == 0, x <= 1)
+
+    class Edge:
+        def __init__(self, d, onward, back, behind, conditions):
+            self.sends, self.takes, self.wraps, self.wrapped, self.passed = conditions
+            self.copy = s.make(kv.at[d, x], kv.at[d, x], onward)
+            self.wrap = s.make(kv.at[d, x], kv.at[d, x], back)
+            self.onward = s.make(kv.at[d, behind], kv.at[d, behind], onward)
+
+        def begin(self):
+            pl.when(self.sends)(self.copy.start)
+            pl.when(self.wraps)(self.wrap.start)
+
+        def hand_on(self):
+            pl.when(self.takes)(self.copy.wait_recv)
+            pl.when(inner)(self.onward.start)
+
+        def near(self):
+            pl.when(self.wrapped)(self.wrap.wait_recv)
+
+        def rest(self):
+            pl.when(self.passed)(self.onward.wait_recv)
+
+        def end(self):
+            pl.when(self.sends)(self.copy.wait_send)
+            pl.when(self.wraps)(self.wrap.wait_send)
+            pl.when(inner)(self.onward.wait_send)
+
+    top = Edge(0, p.xp, p.xm, p.xs[3], first_row)
+    bottom = Edge(4, p.xm, p.xp, p.xs[1], last_row)
+    top.begin()
+    w_from_below(3)
 
     for pair in (far0, far1[0], far1[1], far2[0], far2[1], far3[0], far3[1], far4):
         settle(pair)
@@ -295,7 +365,10 @@
         down.wait_recv()
         if d < 4:
             down = s.start(kv.at[d, x], kv.at[d + 1, x], p.nextrow)
-        side[d] = both(kv.at[d, x])
+        if d < 4:
+            side[d] = both(kv.at[d, x])
+        else:
+            bottom.begin()
 
     def take_side(d):
         side[d][0].wait_recv()
@@ -303,124 +376,89 @@
         side[d][1].wait_recv()
         far[d] = (one, s.same(kv.at[d, p.xs[1], pl.ds(64, 64)], p.xm))
 
-    def take_far(d):
+    def end_row(d):
         settle(far[d])
 
-    w_forward(1)
+    def edge(k):
+        xx = p.xs[k]
+        attend(4 * lax.div(xx - x + 3, 4), xx)
+
     attend(0, x, diagonal=True)
     take_down(1)
-    take_side(0)
+    w_from_above(1)
     attend(1, x)
-    w_forward(2)
     take_down(2)
+    top.hand_on()
+    w_from_above(2)
     attend(2, x)
     take_side(1)
     attend(1, p.xs[3])
     attend(1, p.xs[1])
     take_down(3)
+    w_from_above(3)
     attend(3, x)
-    w_forward(3)
     take_side(2)
-    take_far(1)
+    end_row(1)
     attend(1, p.xs[2])
     attend(2, p.xs[3])
     attend(2, p.xs[1])
     take_down(4)
+    w_from_above(4)
     attend(4, x)
     take_side(3)
-    take_far(2)
+    end_row(2)
     attend(2, p.xs[2])
-    settle(w_z)
-    w_up(p.zs[4])
     attend(3, p.xs[3])
     attend(3, p.xs[1])
-    take_side(4)
-    take_far(3)
+    bottom.hand_on()
+    end_row(3)
     attend(3, p.xs[2])
-    take_far(0)
-
-    def edge(k):
-        xx = p.xs[k]
-        attend(4 * lax.div(xx - x + 3, 4), xx)
-
+    top.near()
+    bottom.near()
     edge(3)
     edge(1)
-    take_far(4)
-    edge(2)
-
-    for j in range(QH):
-        for t in range(4):
-            at = slice(j * BLK + t * PIECE, j * BLK + (t + 1) * PIECE)
-            part = acc[:HEAD, at] * (1.0 / acc[HEAD : HEAD + 1, at])
-            mixed[t * PIECE : (t + 1) * PIECE, j * HEAD : (j + 1) * HEAD] = part.T.astype(BF16)
     for copy in w_y:
         copy.wait_recv()
-    s.drain()
-
-
-def attention(tokens, wq, wkv, wout, cos, sin, start):
-    vmem = pl.BlockSpec(memory_space=pltpu.VMEM)
-    hbm = pl.BlockSpec(memory_space=pltpu.HBM)
-    return pl.pallas_call(
-        attention_kernel,
-        out_shape=(
-            jax.ShapeDtypeStruct((BLK, QH * HEAD), BF16),
-            jax.ShapeDtypeStruct((NYL, NZ, NX, 8, WIDTH), BF16),
-        ),
-        in_specs=[hbm, hbm, hbm, hbm, vmem, vmem, vmem],
-        out_specs=(vmem, vmem),
-        scratch_shapes=[
-            pltpu.VMEM((PIECE, WIDTH), BF16),
-            pltpu.VMEM((4, PIECE, WIDTH), BF16),
-            pltpu.VMEM((64, WIDTH), BF16),
-            pltpu.VMEM((64, WIDTH), BF16),
-            pltpu.VMEM((NYL, NZ, NX, 64, 512), BF16),
-            pltpu.VMEM((NYL, NZ, NX, 64, 256), BF16),
-            pltpu.VMEM((BLK, 768), F32),
-            pltpu.VMEM((HEAD, QH * BLK), BF16),
-            pltpu.VMEM((5, NX, HEAD, 2 * BLK), BF16),
-            pltpu.VMEM((HEAD + 16, QH * BLK), F32),
-            pltpu.VMEM((1, QH * BLK), F32),
-            pltpu.SemaphoreType.DMA((4,)),
-            pltpu.SemaphoreType.DMA((112,)),
-            pltpu.SemaphoreType.DMA((112,)),
-        ],
-        compiler_params=pltpu.CompilerParams(
-            collective_id=1, has_side_effects=True, vmem_limit_bytes=36 << 20
-        ),
-        name="attention",
-    )(tokens, wq, wkv, wout, cos, sin, start)
-
-
-NCHUNK, CHUNK = 8, 512
-
-
-def output_kernel(
-    mixed, w, out, give_far, take_far, own_far, sum_far, via, got, give_near, take_near, own,
-    send_sem, recv_sem,
-):
-    p = Place()
-    other = p.h + 1 - 2 * p.c
+
+    def flatten(g, carry):
+        rows = pl.ds(pl.multiple_of(g * 32, 32), 32)
+        w[rows, :] = wout[lax.div(g, NZ), lax.rem(g, NZ)].reshape(32, WIDTH)
+        return carry
+
+    lax.fori_loop(0, NYL * NZ, flatten, 0)
+    top.rest()
+    bottom.rest()
+    edge(2)
+
+    other = h + 1 - 2 * p.c
     far_other = lax.rem(other + 2, 4)
-    meet([p.yp, p.ym, p.core])
-    s = Sends(send_sem, recv_sem)
+
+    def piece(owner):
+        return pl.ds(pl.multiple_of(owner * PIECE, PIECE), PIECE)
+
+    def mix(owner):
+        for j in range(QH):
+            at = pl.ds(pl.multiple_of(j * BLK + owner * PIECE, PIECE), PIECE)
+            part = acc[:HEAD, at] * (1.0 / acc[HEAD : HEAD + 1, at])
+            mixed[piece(owner), j * HEAD : (j + 1) * HEAD] = part.T.astype(BF16)
 
     def times(owner, n):
-        rows = pl.ds(pl.multiple_of(owner * PIECE, PIECE), PIECE)
         return jnp.dot(
-            mixed[rows, :], w[:, n * CHUNK : (n + 1) * CHUNK], preferred_element_type=F32
+            mixed[piece(owner), :], w[:, n * CHUNK : (n + 1) * CHUNK], preferred_element_type=F32
         )
 
     def toward(n):
         return p.yp if n % 2 == 0 else p.ym
 
-    to_core, hops, near = [], [], []
+    to_core, hops, near, last = [], [], [], []
 
     def combine(n):
         to_core[n].wait_recv()
         sum_far[n] = (own_far[n] + take_far[n].astype(F32)).astype(BF16)
         hops.append(s.start(sum_far.at[n], via.at[n], toward(n)))
 
+    mix(far_other)
+    mix(p.far)
     for n in range(NCHUNK):
         give_far[n] = times(far_other, n).astype(BF16)
         to_core.append(s.start(give_far.at[n], take_far.at[n], p.core))
@@ -429,60 +467,76 @@
             combine(n - 2)
     combine(NCHUNK - 2)
     combine(NCHUNK - 1)
+    mix(other)
+    mix(h)
     for n in range(NCHUNK):
         give_near[n] = times(other, n).astype(BF16)
         near.append(s.start(give_near.at[n], take_near.at[n], p.core))
-        own[n] = times(p.h, n)
-    last = []
+        near_sum[n] = times(h, n)
     for n in range(NCHUNK):
         hops[n].wait_recv()
         last.append(s.start(via.at[n], got.at[n], toward(n)))
     for n in range(NCHUNK):
         near[n].wait_recv()
-        own[n] += take_near[n].astype(F32)
+        near_sum[n] += take_near[n].astype(F32)
     for n in range(NCHUNK):
         last[n].wait_recv()
-        out[:, n * CHUNK : (n + 1) * CHUNK] = (own[n] + got[n].astype(F32)).astype(BF16)
+        out[:, n * CHUNK : (n + 1) * CHUNK] = (near_sum[n] + got[n].astype(F32)).astype(BF16)
     s.drain()
-
-
-def project_out(mixed, w):
+    top.end()
+    bottom.end()
+
+
+NCHUNK, CHUNK = 8, 512
+
+
+def layer(docs, tokens, wq, wkv, wout, freqs):
     vmem = pl.BlockSpec(memory_space=pltpu.VMEM)
+    hbm = pl.BlockSpec(memory_space=pl.ANY)
     piece = pltpu.VMEM((NCHUNK, PIECE, CHUNK), BF16)
     wide = pltpu.VMEM((NCHUNK, PIECE, CHUNK), F32)
     return pl.pallas_call(
-        output_kernel,
+        layer_kernel,
         out_shape=jax.ShapeDtypeStruct((PIECE, WIDTH), BF16),
-        in_specs=[vmem, vmem],
+        in_specs=[pl.BlockSpec(memory_space=pltpu.SMEM), hbm, hbm, hbm, hbm, vmem],
         out_specs=vmem,
         scratch_shapes=[
+            pltpu.VMEM((PIECE, WIDTH), BF16),
+            pltpu.VMEM((4, PIECE, WIDTH), BF16),
+            pltpu.VMEM((64, WIDTH), BF16),
+            pltpu.VMEM((64, WIDTH), BF16),
+            pltpu.VMEM((NYL, NZ, NX, 64, 512), BF16),
+            pltpu.VMEM((NYL, NZ, NX, 64, 256), BF16),
+            pltpu.VMEM((NYL, NZ, NX, 8, WIDTH), BF16),
+            pltpu.VMEM((BLK, HEAD), F32),
+            pltpu.VMEM((BLK, HEAD), F32),
+            pltpu.VMEM((1, BLK), jnp.int32),
+            pltpu.VMEM((BLK, 768), F32),
+            pltpu.VMEM((HEAD, QH * BLK), BF16),
+            pltpu.VMEM((5, NX, HEAD, 2 * BLK), BF16),
+            pltpu.VMEM((HEAD + 16, QH * BLK), F32),
+            pltpu.VMEM((1, QH * BLK), F32),
+            pltpu.VMEM((BLK, WIDTH), BF16),
+            pltpu.VMEM((BLK, QH * HEAD), BF16),
             piece, piece, wide, piece, piece, piece, piece, piece, wide,
-            pltpu.SemaphoreType.DMA((32,)),
-            pltpu.SemaphoreType.DMA((32,)),
+            pltpu.SemaphoreType.DMA((4,)),
+            pltpu.SemaphoreType.DMA((160,)),
+            pltpu.SemaphoreType.DMA((160,)),
         ],
         compiler_params=pltpu.CompilerParams(
-            collective_id=3, has_side_effects=True, vmem_limit_bytes=48 << 20
+            collective_id=1, has_side_effects=True, vmem_limit_bytes=60 << 20
         ),
-        name="output",
-    )(mixed, w)
+        name="layer",
+    )(docs, tokens, wq, wkv, wout, freqs)
 
 
 def on_device(tokens, w_query, key_value_weight, w_out, doc_lengths):
-    blk_index = lax.axis_index("blk")
-    positions = blk_index * BLK + jnp.arange(BLK, dtype=jnp.int32)
-    ends = jnp.cumsum(doc_lengths)
-    after = positions[:, None] >= ends[None, :]
-    starts = jnp.sum(jnp.where(after, doc_lengths[None, :], 0), axis=1).astype(jnp.int32)
     half = HEAD // 2
     freqs = jnp.power(rope_base, -2.0 * jnp.arange(half, dtype=F32) / HEAD)
-    angle = (positions - starts).astype(F32)[:, None] * freqs[None, :]
-    cosine, sine = jnp.cos(angle), jnp.sin(angle)
-    cos2 = jnp.concatenate([cosine, cosine], axis=1)
-    sin2 = jnp.concatenate([-sine, sine], axis=1)
-    mixed, head_rows = attention(
-        tokens, w_query, key_value_weight.reshape(64, 256), w_out, cos2, sin2, starts[None, :]
+    freqs = jnp.concatenate([freqs, freqs])[None, :]
+    return layer(
+        doc_lengths, tokens, w_query, key_value_weight.reshape(64, 256), w_out, freqs
     )
-    return project_out(mixed, head_rows.reshape(512, WIDTH))
 
 
 def solution(mesh):

time: 154 us -> 147 us (0.955)
  Pallas kernels: 146 us -> 142 us
  local copies, waits for them, and re-layouts: 5.37 us -> 3.66 us
    pallas_call x2 -> x1, Pallas kernels: 146 us -> 142 us  [layer(): pl.pallas_call(layer_kernel, out_shape=jax.ShapeDtypeStruct((PIECE, WIDTH...]
    unnamed x8 -> x2, local copies, waits for them, and re-layouts: 4.64 us -> 3.66 us
where the time goes in v4:
time: 147 us
  Pallas kernels  142 us (97%)
  local copies, waits for them, and re-layouts  3.66 us (2%)
    pallas_call x1, Pallas kernels, layer(): pl.pallas_call(layer_kernel, out_shape=jax.ShapeDtypeStruct((PIECE, WIDTH...  142 us
    unnamed x2, local copies, waits for them, and re-layouts  3.66 us

profile of v4, /device:TPU:1, one launch (start us, length us, event | category | flops | bytes accessed | tf_op | source)
XLA Modules:
  0.0 146.6 jit_solution(2745653995722481068)
XLA Ops:
  0.0 0.7 maximum_bitcast_fusion.freqs
  0.7 1.4 copy.8
  2.1 142.3 %layer.1 = bf16[128,4096]{1,0:T(8,128)(2,1)} custom-call(s32[16]{0:T(128)} %docs.1, bf16[128,4096]{1,0:T(8,128)(2,1)} %tokens_in.1, bf16[64,512]{1,0:T(8,128)(2,1)} %wq_in.1, bf16[64,256]{1,0:T(8,128)(2,1)} %bitcast.6, bf16[8,4096]{1,0:T(8,128)(2,1)} %wout_in.1, f32[1,128]{1,0:T(1,128)} %maximum_bitcast_fusion.freqs), custom_call_target="tpu_custom_call" | custom-call | tf_op jit(solution)/shard_map/layer/pallas_call | solution.py:498
  144.4 2.3 %copy.10 = bf16[128,4096]{1,0:T(8,128)(2,1)} copy(bf16[128,4096]{1,0:T(8,128)(2,1)} %layer.1) | data formatting | bytes 2097152
  (1 shorter events, 0.0 us)
